TPU v7x, 128 devices: a whole 4x4x4 slice. The times are simulated.
128 devices in a mesh: cell: 8 (over z, core), tm: 16 (over y, x).
Axes of the slice: x: 4, y: 4, z: 4, core: 2. Of those that a mesh axis runs over, the one named last changes fastest.
Arguments:
- solution: float32 [32768], P(('cell', 'tm')), may hold values from -6 to 6
- residual: float32 [32768], P(('cell', 'tm')), may hold values from -8 to 8
- direction: float32 [32768], P(('cell', 'tm')), may hold values from -8 to 8
- noise_var: float32 [32768], P(('cell', 'tm')), may hold values from 0.5 to 2
- footprints: bfloat16 [262144, 128], P(('cell', 'tm')), may hold values from -0.5 to 0.5
- tile_owner: int32 [262144, 1], P(('cell', 'tm')), may hold values from 0 to 127; in each aligned block of 2048 rows (0 to 2047, 2048 to 4095, ...) at most 32 rows name the same one
- tile_block: int32 [262144], P(('cell', 'tm')), may hold values from 0 to 8
- tile_step: int32 [262144], P(('cell', 'tm')), may hold values from 0 to 127
- tile_obs: int32 [262144], P(('cell', 'tm')), may hold values from 0 to 255
- cell_cov: bfloat16 [9216, 9216], P('cell'), may hold values from -2 to 7, as said below
- time_cov: bfloat16 [2048, 2048], P('tm'), may hold values from -2 to 7, as said below
Outputs:
- new_solution: float32 [32768], P(('cell', 'tm'))
- new_residual: float32 [32768], P(('cell', 'tm'))
- new_direction: float32 [32768], P(('cell', 'tm'))
Inputs may be any that keep to these rules, and one draw needn't show every extreme that they name: `tile_owner`: among the 2048 tiles of one device, no owner is named by more than 32 of them. `cell_cov`: symmetric positive definite. `time_cov`: symmetric positive definite.
All inputs are finite; a program needn't handle non-finite values.
Results may differ from a plain program's by a relative error of at most 0.0021.
Values may be sent and summed in bfloat16 or wider, within the bound.
A program may use at most 128 MiB of HBM per device.

v0:
```python
import functools

import jax
import jax.numpy as jnp
from jax import lax
from jax.sharding import Mesh
from jax.sharding import PartitionSpec as P

CELL = ("cell_0", "cell_1")
TM = ("tm_0", "tm_1")
CELL_TM = ("cell_0", "cell_1", "tm_0", "tm_1")


def laid_out(pieces, dim):
    lengths = list(pieces.shape[1:])
    lengths[dim] *= pieces.shape[0]
    return jnp.moveaxis(pieces, 0, dim).reshape(lengths)


def from_everyone(value, axis):
    peers = lax.axis_size(axis)
    return lax.all_to_all(
        jnp.broadcast_to(value[None], (peers, *value.shape)), axis, 0, 0, tiled=True
    )


def collect(value, axis, dim):
    return laid_out(from_everyone(value, axis), dim)


def over_axes(value, axes):
    return functools.reduce(lax.psum, axes, value)


def local(
    solution,
    residual,
    direction,
    noise_var,
    footprints,
    tile_owner,
    tile_block,
    tile_step,
    tile_obs,
    cell_cov,
    time_cov,
):
    devices = lax.axis_size(CELL) * lax.axis_size(TM)
    tile_count = footprints.shape[0]
    block_len = footprints.shape[1]
    cell_local = cell_cov.shape[0]
    time_local = time_cov.shape[0]
    block_local = cell_local // block_len
    obs_local = direction.shape[0]
    capacity = max(2, 2 * tile_count // devices)
    slot_total = devices * capacity
    owner_dev = tile_owner[:, 0]
    owner_hot = (owner_dev[:, None] == jnp.arange(devices, dtype=jnp.int32)[None, :]).astype(
        jnp.int32
    )
    slot_rank = jnp.sum(jnp.cumsum(owner_hot, axis=0) * owner_hot, axis=1) - 1
    slot_index = owner_dev * capacity + slot_rank
    obs_hot = (tile_obs[:, None] == jnp.arange(obs_local, dtype=jnp.int32)[None, :]).astype(
        jnp.float32
    )
    dir_tile = jnp.dot(obs_hot, direction, precision=lax.Precision.HIGHEST).astype(jnp.bfloat16)
    tile_place = tile_step * block_local + tile_block
    send_values = jnp.zeros((slot_total, block_len), jnp.bfloat16).at[slot_index].set(footprints)
    send_dir = jnp.zeros((slot_total,), jnp.bfloat16).at[slot_index].set(dir_tile)
    send_place = jnp.zeros((slot_total,), jnp.int32).at[slot_index].set(tile_place)
    got_values, got_dir, got_place = (
        lax.all_to_all(
            send_values.reshape(devices, capacity, block_len),
            CELL_TM,
            split_axis=0,
            concat_axis=0,
            tiled=True,
        ),
        lax.all_to_all(
            send_dir.reshape(devices, capacity), CELL_TM, split_axis=0, concat_axis=0, tiled=True
        ),
        lax.all_to_all(
            send_place.reshape(devices, capacity), CELL_TM, split_axis=0, concat_axis=0, tiled=True
        ),
    )
    got_values = got_values.reshape(slot_total, block_len).astype(jnp.float32)
    got_dir = got_dir.reshape(slot_total).astype(jnp.float32)
    got_place = got_place.reshape(slot_total)
    flux_time = jnp.zeros((time_local * block_local, block_len), jnp.float32)
    flux_time = flux_time.at[got_place].add(got_dir[:, None] * got_values)
    flux_grid = flux_time.reshape(time_local, cell_local).T.astype(jnp.bfloat16)
    mixed_cells = jnp.dot(
        cell_cov, collect(flux_grid, CELL, 0), preferred_element_type=jnp.float32
    ).astype(jnp.bfloat16)
    smoothed = lax.dot_general(
        time_cov,
        lax.all_gather(mixed_cells, TM, axis=1, tiled=True),
        (((1,), (1,)), ((), ())),
        preferred_element_type=jnp.float32,
    )
    smoothed = smoothed.astype(jnp.bfloat16).reshape(time_local * block_local, block_len)
    slot_dots = jnp.sum(got_values * smoothed[got_place].astype(jnp.float32), axis=1)
    returned = lax.all_to_all(
        slot_dots.reshape(devices, capacity), CELL_TM, split_axis=0, concat_axis=0, tiled=True
    )
    tile_dots = returned.reshape(slot_total)[slot_index]
    applied = jnp.dot(tile_dots, obs_hot, precision=lax.Precision.HIGHEST) + noise_var * direction
    norm_now, curvature, cross_term, image_norm = (
        over_axes(jnp.sum(residual * residual), CELL_TM),
        over_axes(jnp.sum(direction * applied), CELL_TM),
        over_axes(jnp.sum(residual * applied), CELL_TM),
        over_axes(jnp.sum(applied * applied), CELL_TM),
    )
    step_size = norm_now / curvature
    new_solution = solution + step_size * direction
    new_residual = residual - step_size * applied
    norm_next = norm_now - 2.0 * step_size * cross_term + step_size * step_size * image_norm
    new_direction = new_residual + norm_next / norm_now * direction
    return (new_solution, new_residual, new_direction)


def solution(mesh):
    finer = Mesh(mesh.devices.reshape(4, 2, 4, 4), ("cell_0", "cell_1", "tm_0", "tm_1"))
    in_specs = (
        P(CELL_TM),
        P(CELL_TM),
        P(CELL_TM),
        P(CELL_TM),
        P(CELL_TM, None),
        P(CELL_TM, None),
        P(CELL_TM),
        P(CELL_TM),
        P(CELL_TM),
        P(CELL, None),
        P(TM, None),
    )
    out_specs = (P(CELL_TM), P(CELL_TM), P(CELL_TM))
    return jax.shard_map(local, mesh=finer, in_specs=in_specs, out_specs=out_specs, check_vma=False)
```

profile of v0, /device:TPU:1, one launch (start us, length us, event | category | flops | bytes accessed | tf_op | source)
XLA Modules:
  0.0 302.6 jit_solution(9273110876222847107)
XLA Ops:
  7.2 0.9 copy.20
  8.0 0.3 fusion.8
  8.6 0.3 copy.21
  8.9 0.2 copy-done.1
  9.1 0.6 fusion.5
  9.8 1.0 fusion.4
  10.9 14.6 %scatter_custom_fusion.2 = bf16[4096]{0:T(1024)(128)(2,1)S(1)} fusion(s32[2048]{0:T(1024)S(1)} %bitcast.43, bf16[2048]{0:T(1024)(128)(2,1)S(1)} %convert_element_type.58, bf16[]{:T(256)} %constant.10.clone.1), kind=kCustom, calls=%fused_computation.39 | custom fusion | bytes 8194 | tf_op jit(solution)/shard_map/scatter | solution.py:69
  25.5 0.7 all_to_all.32
  26.2 11.5 %all-to-all-start.2 = ((bf16[128,1,32]{2,1,0:T(2,128)(2,1)}), bf16[128,1,32]{2,1,0:T(2,128)(2,1)S(1)}, u32[]{:S(2)}, u32[]{:S(2)}) async-start(bf16[128,1,32]{2,1,0:T(2,128)(2,1)} %all_to_all.32), calls=%async_computation.2 | async-start | bytes 131072 | tf_op jit(solution)/shard_map/all_to_all | solution.py:79
  37.7 8.1 %scatter_custom_fusion.1 = s32[4096]{0:T(1024)S(1)} fusion(s32[2048]{0:T(1024)S(1)} %bitcast.44, s32[2048]{0:T(1024)S(1)} %multiply_add_fusion, s32[]{:T(128)} %constant.12.clone.1), kind=kCustom, calls=%fused_computation.36 | custom fusion | bytes 16388 | tf_op jit(solution)/shard_map/scatter | solution.py:70
  45.8 0.7 all_to_all.25
  46.5 0.8 all-to-all-done.2
  47.3 8.9 %all-to-all-start.1 = ((s32[128,1,32]{2,1,0:T(1,128)}), s32[128,1,32]{2,1,0:T(1,128)S(1)}, u32[]{:S(2)}, u32[]{:S(2)}) async-start(s32[128,1,32]{2,1,0:T(1,128)} %bitcast.8), calls=%async_computation.1 | async-start | bytes 131072 | tf_op jit(solution)/shard_map/all_to_all | solution.py:82
  56.3 7.2 %scatter_custom_fusion = bf16[4096,128]{1,0:T(8,128)(2,1)} fusion(s32[2048]{0:T(1024)S(1)} %bitcast.45, bf16[2048,128]{1,0:T(8,128)(2,1)} %param.15, bf16[]{:T(256)} %constant.10.clone.1), kind=kCustom, calls=%fused_computation.26 | custom fusion | bytes 1049088 | tf_op jit(solution)/shard_map/scatter | solution.py:68
  63.4 2.5 all-to-all-done.1
  65.9 7.3 %all-to-all-start = ((bf16[128,32,128]{2,1,0:T(8,128)(2,1)}), bf16[128,32,128]{2,1,0:T(8,128)(2,1)S(1)}, u32[]{:S(2)}, u32[]{:S(2)}) async-start(bf16[128,32,128]{2,1,0:T(8,128)(2,1)} %bitcast.7), calls=%async_computation | async-start | bytes 2097152 | tf_op jit(solution)/shard_map/all_to_all | solution.py:72
  73.2 0.2 all-gather.2.cloned.1.call-start
  73.4 0.2 convert_reduce_fusion
  73.6 0.1 reshape.115
  73.7 0.5 broadcast.93
  74.2 0.8 reduce.11
  75.0 0.1 reshape.111
  75.1 16.9 %all-to-all-done = bf16[128,32,128]{2,1,0:T(8,128)(2,1)S(1)} async-done(((bf16[128,32,128]{2,1,0:T(8,128)(2,1)}), bf16[128,32,128]{2,1,0:T(8,128)(2,1)S(1)}, u32[]{:S(2)}, u32[]{:S(2)}) %all-to-all-start) | async-done | bytes 1048608 | tf_op jit(solution)/shard_map/all_to_all | solution.py:72
  92.1 2.0 bitcast_multiply_fusion
  94.0 22.9 %scatter_custom_fusion.3 = f32[1152,128]{1,0:T(8,128)S(1)} fusion(s32[4096]{0:T(1024)S(1)} %bitcast.41, f32[4096,128]{1,0:T(8,128)} %bitcast_multiply_fusion, f32[]{:T(128)} %constant.9.clone.1), kind=kCustom, calls=%fused_computation.28 | custom fusion | flops 524288 | bytes 590336 | tf_op jit(solution)/shard_map/scatter-add | solution.py:90
  117.0 0.4 convert_element_type.64
  117.3 0.2 copy.24
  117.6 0.3 broadcast_in_dim.11
  117.9 33.4 %all_to_all.38 = bf16[8,1152,128]{2,1,0:T(8,128)(2,1)S(1)} all-to-all(bf16[8,1152,128]{2,1,0:T(8,128)(2,1)S(1)} %broadcast_in_dim.11), channel_id=1, replica_groups=mesh['cell_0'=4,'cell_1'=2,'tm_0'=4,'tm_1'=4] {'cell_0','cell_1'}, dimensions={0} | all-to-all | bytes 4718592 | tf_op jit(solution)/shard_map/all_to_all | solution.py:22
  151.3 11.7 %fusion.1 = bf16[1152,128]{0,1:T(8,128)(2,1)} fusion(bf16[9216,128]{1,0:T(8,128)(2,1)S(1)} %bitcast.36, bf16[1152,9216]{1,0:T(8,128)(2,1)} %param.20), kind=kOutput, calls=%fused_computation.9 | convolution fusion | flops 2718056448 | bytes 23887872 | tf_op jit(solution)/shard_map/dot_general | solution.py:92
  163.0 50.4 %all-gather.2.cloned.1.call-done = bf16[1152,2048]{0,1:T(8,128)(2,1)} async-done(((bf16[1152,128]{0,1:T(8,128)(2,1)}), bf16[1152,2048]{0,1:T(8,128)(2,1)}) %all-gather.2.cloned.1.call-update) | async-done | bytes 4718608 | tf_op jit(solution)/shard_map/all_gather | solution.py:97
  213.4 3.8 %fusion = bf16[128,1152]{0,1:T(8,128)(2,1)S(1)} fusion(bf16[1152,2048]{0,1:T(8,128)(2,1)} %all-gather.2.cloned.1.call-done, bf16[128,2048]{1,0:T(8,128)(2,1)S(1)} %copy-done), kind=kOutput, calls=%fused_computation.8 | convolution fusion | flops 604127232 | bytes 5537792 | tf_op jit(solution)/shard_map/dot_general | solution.py:95
  217.1 0.2 copy.25
  217.4 0.3 reshape.113
  217.7 12.1 %gather_fusion = bf16[4096,128]{1,0:T(8,128)(2,1)S(1)} fusion(bf16[1152,128]{1,0:T(8,128)(2,1)S(1)} %reshape.113, s32[4096]{0:T(1024)S(1)} %broadcast_clamp_fusion), kind=kCustom, calls=%fused_computation | custom fusion | bytes 2113536 | tf_op jit(solution)/shard_map/gather | solution.py:102
  229.8 1.3 fusion.2
  231.1 8.2 %all-to-all-start.4 = ((f32[128,1,32]{2,1,0:T(1,128)}), f32[128,1,32]{2,1,0:T(1,128)S(1)}, u32[]{:S(2)}, u32[]{:S(2)}) async-start(f32[128,1,32]{2,1,0:T(1,128)} %bitcast.18), calls=%async_computation.4 | async-start | bytes 131072 | tf_op jit(solution)/shard_map/all_to_all | solution.py:103
  239.3 9.6 %all-to-all-done.4 = f32[128,1,32]{2,1,0:T(1,128)S(1)} async-done(((f32[128,1,32]{2,1,0:T(1,128)}), f32[128,1,32]{2,1,0:T(1,128)S(1)}, u32[]{:S(2)}, u32[]{:S(2)}) %all-to-all-start.4) | async-done | bytes 16416 | tf_op jit(solution)/shard_map/all_to_all | solution.py:103
  248.9 0.5 broadcast.94
  249.4 0.8 reduce.12
  250.3 11.8 %gather_fusion.1 = f32[2048]{0:T(1024)S(1)} fusion(f32[4096]{0:T(1024)S(1)} %reshape.114, s32[2048]{0:T(1024)S(1)} %broadcast_clamp_fusion.1), kind=kCustom, calls=%fused_computation.1 | custom fusion | bytes 24576 | tf_op jit(solution)/shard_map/gather | solution.py:106
  262.1 0.8 fusion.3
  262.9 0.6 multiply_reduce_fusion
  263.5 7.4 %all-reduce.2 = (f32[]{:T(128)}, f32[]{:T(128)}, f32[]{:T(128)}, f32[]{:T(128)}) all-reduce(f32[]{:T(128)} %get-tuple-element.5, f32[]{:T(128)} %get-tuple-element.6, f32[]{:T(128)} %get-tuple-element.4, f32[]{:T(128)} %get-tuple-element.3), channel_id=1, replica_groups=mesh['cell_0'=4,'cell_1'=2,'tm_0'=4,'tm_1'=4] {'cell_0'}, use_global_device_ids=true, to_apply=%region_1.2 | all-reduce | flops 4 | bytes 32 | tf_op jit(solution)/shard_map/psum | solution.py:32
  270.9 5.6 %all-reduce.3 = (f32[]{:T(128)}, f32[]{:T(128)}, f32[]{:T(128)}, f32[]{:T(128)}) all-reduce(f32[]{:T(128)} %get-tuple-element.15, f32[]{:T(128)} %get-tuple-element.16, f32[]{:T(128)} %get-tuple-element.17, f32[]{:T(128)} %get-tuple-element.18), channel_id=1, replica_groups=mesh['cell_0'=4,'cell_1'=2,'tm_0'=4,'tm_1'=4] {'cell_1'}, use_global_device_ids=true, to_apply=%region_2.3 | all-reduce | flops 4 | bytes 32 | tf_op jit(solution)/shard_map/psum | solution.py:32
  276.5 7.1 %all-reduce.1 = (f32[]{:T(128)}, f32[]{:T(128)}, f32[]{:T(128)}, f32[]{:T(128)}) all-reduce(f32[]{:T(128)} %get-tuple-element.19, f32[]{:T(128)} %get-tuple-element.20, f32[]{:T(128)} %get-tuple-element.21, f32[]{:T(128)} %get-tuple-element.22), channel_id=1, replica_groups=mesh['cell_0'=4,'cell_1'=2,'tm_0'=4,'tm_1'=4] {'tm_0'}, use_global_device_ids=true, to_apply=%region_3.4 | all-reduce | flops 4 | bytes 32 | tf_op jit(solution)/shard_map/psum | solution.py:32
  283.6 7.7 %all-reduce = (f32[]{:T(128)}, f32[]{:T(128)}, f32[]{:T(128)}, f32[]{:T(128)}) all-reduce(f32[]{:T(128)} %get-tuple-element.11, f32[]{:T(128)} %get-tuple-element.12, f32[]{:T(128)} %get-tuple-element.13, f32[]{:T(128)} %get-tuple-element.14), channel_id=1, replica_groups=mesh['cell_0'=4,'cell_1'=2,'tm_0'=4,'tm_1'=4] {'tm_1'}, use_global_device_ids=true, to_apply=%region_4.5 | all-reduce | flops 4 | bytes 32 | tf_op jit(solution)/shard_map/psum | solution.py:32
  295.1 0.6 multiply_add_fusion.1
  (31 shorter events, 0.4 us)
Async XLA Ops:
  7.2 206.2 %copy-start = (bf16[128,2048]{1,0:T(8,128)(2,1)S(1)}, bf16[128,2048]{1,0:T(8,128)(2,1)}, u32[]{:S(2)}) copy-start(bf16[128,2048]{1,0:T(8,128)(2,1)} %param.21) | copy-start | bytes 1572868
  8.4 0.7 copy-start.1
  8.5 1.3 copy-start.4
  8.5 1.3 copy-start.8
  8.5 29.1 %copy-start.2 = (s32[2048]{0:T(1024)S(1)}, s32[2048]{0:T(1024)}, u32[]{:S(2)}) copy-start(s32[2048]{0:T(1024)} %param.17) | copy-start | bytes 24580
  8.6 29.1 %copy-start.3 = (s32[2048]{0:T(1024)S(1)}, s32[2048]{0:T(1024)}, u32[]{:S(2)}) copy-start(s32[2048]{0:T(1024)} %param.18) | copy-start | bytes 24580
  26.2 21.1 %all-to-all-start.2 = ((bf16[128,1,32]{2,1,0:T(2,128)(2,1)}), bf16[128,1,32]{2,1,0:T(2,128)(2,1)S(1)}, u32[]{:S(2)}, u32[]{:S(2)}) async-start(bf16[128,1,32]{2,1,0:T(2,128)(2,1)} %all_to_all.32), calls=%async_computation.2 | async-start | bytes 131072 | tf_op jit(solution)/shard_map/all_to_all | solution.py:79
  47.3 18.6 %all-to-all-start.1 = ((s32[128,1,32]{2,1,0:T(1,128)}), s32[128,1,32]{2,1,0:T(1,128)S(1)}, u32[]{:S(2)}, u32[]{:S(2)}) async-start(s32[128,1,32]{2,1,0:T(1,128)} %bitcast.8), calls=%async_computation.1 | async-start | bytes 131072 | tf_op jit(solution)/shard_map/all_to_all | solution.py:82
  65.9 26.2 %all-to-all-start = ((bf16[128,32,128]{2,1,0:T(8,128)(2,1)}), bf16[128,32,128]{2,1,0:T(8,128)(2,1)S(1)}, u32[]{:S(2)}, u32[]{:S(2)}) async-start(bf16[128,32,128]{2,1,0:T(8,128)(2,1)} %bitcast.7), calls=%async_computation | async-start | bytes 2097152 | tf_op jit(solution)/shard_map/all_to_all | solution.py:72
  73.2 140.2 %all-gather.2.cloned.1.call-start = ((), (), s32[]{:S(2)}) async-start(), calls=%async_computation.5 | async-start | bytes 5013504 | tf_op jit(solution)/shard_map/all_gather | solution.py:97
  231.1 17.8 %all-to-all-start.4 = ((f32[128,1,32]{2,1,0:T(1,128)}), f32[128,1,32]{2,1,0:T(1,128)S(1)}, u32[]{:S(2)}, u32[]{:S(2)}) async-start(f32[128,1,32]{2,1,0:T(1,128)} %bitcast.18), calls=%async_computation.4 | async-start | bytes 131072 | tf_op jit(solution)/shard_map/all_to_all | solution.py:103
  250.3 12.6 %copy-start.5 = (f32[256]{0:T(256)S(1)}, f32[256]{0:T(256)}, u32[]{:S(2)}) copy-start(f32[256]{0:T(256)} %param.12) | copy-start | bytes 3076
  250.3 12.6 %copy-start.6 = (f32[256]{0:T(256)S(1)}, f32[256]{0:T(256)}, u32[]{:S(2)}) copy-start(f32[256]{0:T(256)} %param.14) | copy-start | bytes 3076
  250.3 44.8 %copy-start.7 = (f32[256]{0:T(256)S(1)}, f32[256]{0:T(256)}, u32[]{:S(2)}) copy-start(f32[256]{0:T(256)} %param.11) | copy-start | bytes 3076
Sparse Core Ops, SparseCore 0:
  163.1 50.2 all-gather.1
where the time goes:
time: 306 us; the launch traced here: 303 us
  waiting for transfers between devices  80.2 us (26%)
  blocking collectives  61.1 us (20%)
  local copies, waits for them, and re-layouts  59.3 us (19%)
  starting transfers between devices  36.1 us (12%)
  other arithmetic  30.3 us (10%)
  between operations  18.3 us (6%)
  matrix products  17.3 us (6%)
    all_gather x1, waiting for transfers between devices, local(): lax.all_gather(mixed_cells, TM, axis=1, tiled=True)  50.4 us
    all_to_all x1, blocking collectives, from_everyone(): lax.all_to_all(jnp.broadcast_to(value[None], (peers, *value.shape)), axis...  33.4 us
    psum x4, blocking collectives, over_axes(): return functools.reduce(lax.psum, axes, value)  27.7 us
    scatter-add x1, other arithmetic, local(): flux_time = flux_time.at[got_place].add(got_dir[:, None] * got_values)  22.9 us
    all_to_all x1, waiting for transfers between devices, local(): lax.all_to_all(send_values.reshape(devices, capacity, block_len), CELL_TM...  16.9 us
    scatter x1, local copies, waits for them, and re-layouts, local(): jnp.zeros((slot_total,), jnp.bfloat16).at[slot_index].set(dir_tile)  14.6 us
    gather x1, local copies, waits for them, and re-layouts, local(): smoothed[got_place].astype(jnp.float32)  12.1 us
    gather x1, local copies, waits for them, and re-layouts, local(): tile_dots = returned.reshape(slot_total)[slot_index]  11.8 us
  transfers between devices with their start and end apart: 5, of which 5 were waited for; matrix products, arithmetic and copies ran while one was open for 6% of the time, Pallas kernels for 0%

commit v1 on v0

v1 whole, which is shorter than its diff:
```python
import functools

import jax
import jax.numpy as jnp
from jax import lax
from jax.experimental import pallas as pl
from jax.experimental.pallas import tpu as pltpu
from jax.sharding import PartitionSpec as P

MESH = pl.DeviceIdType.MESH
HIGHEST = lax.Precision.HIGHEST
CELL_TM = ("cell", "tm")
NN = (((1,), (0,)), ((), ()))
NT = (((1,), (1,)), ((), ()))
DEV = 128
CAP = 32
LANES = 128
OBS = 256
TILES = 2048
SLOTS = DEV * CAP
ROWS = 1152
BLOCKS = 9
HALF = ROWS // 2
QUARTER = ROWS // 4
BF16 = jnp.bfloat16
F32 = jnp.float32


def mul(a, b, dims=NN, precision=None):
    return lax.dot_general(a, b, dims, precision=precision, preferred_element_type=F32)


def sub_iota(rows, cols):
    return lax.broadcasted_iota(jnp.int32, (rows, cols), 0)


def hot_of(index, rows):
    return jnp.where(sub_iota(rows, index.shape[1]) == index, 1.0, 0.0)


def prep_kernel(
    owner_ref,
    block_ref,
    step_ref,
    obs_ref,
    dir_ref,
    foot_ref,
    values_ref,
    meta_ref,
    lane_ref,
    slot_vmem,
    slot_smem,
    wide,
    slots,
    sem,
):
    lane_base = (lax.axis_index("cell") * 16 + lax.axis_index("tm")) % 4 * CAP
    width = 256
    above = jnp.where(
        sub_iota(width, width) < lax.broadcasted_iota(jnp.int32, (width, width), 1), 1.0, 0.0
    ).astype(BF16)
    carry = jnp.zeros((DEV, 1), F32)
    ranks = []
    for at in range(0, TILES, width):
        hot = hot_of(owner_ref[:, at : at + width], DEV)
        before = mul(hot.astype(BF16), above) + carry
        ranks.append(jnp.sum(hot * before, axis=0, keepdims=True))
        carry = before[:, width - 1 : width] + hot[:, width - 1 : width]
    rank = jnp.concatenate(ranks, axis=1).astype(jnp.int32)
    slot_vmem[...] = owner_ref[...] * CAP + rank
    copy = pltpu.make_async_copy(slot_vmem, slot_smem, sem)
    copy.start()
    wide[...] = foot_ref[...].astype(F32)
    slots[...] = jnp.zeros_like(slots)
    lane = rank + lane_base
    lane_ref[...] = lane
    owner_hot = hot_of(owner_ref[...], DEV).astype(BF16)
    obs_hot = hot_of(obs_ref[...], OBS).astype(BF16)
    dir_row = jnp.broadcast_to(dir_ref[...], (8, OBS)).astype(BF16)
    dir_tile = mul(dir_row, obs_hot)[0:1, :]
    at_lane = sub_iota(LANES, TILES) == lane

    def placed(value):
        return mul(owner_hot, jnp.where(at_lane, value, 0.0).astype(BF16), NT)

    meta_ref[:, 0, :] = placed(dir_tile)
    meta_ref[:, 1, :] = (
        placed(block_ref[...].astype(F32)) * 128.0 + placed(step_ref[...].astype(F32))
    )
    copy.wait()

    def move(group, _):
        for k in range(8):
            i = group * 8 + k
            slots[pl.ds(slot_smem[0, i], 1), :] = wide[pl.ds(i, 1), :]
        return 0

    lax.fori_loop(0, TILES // 8, move, 0, unroll=4)
    values_ref[...] = slots[...].astype(BF16)


def prep(owner, block, step, obs, direction, footprints):
    return pl.pallas_call(
        prep_kernel,
        out_shape=(
            jax.ShapeDtypeStruct((SLOTS, LANES), BF16),
            jax.ShapeDtypeStruct((DEV, 2, LANES), F32),
            jax.ShapeDtypeStruct((1, TILES), jnp.int32),
        ),
        in_specs=[pl.BlockSpec(memory_space=pltpu.VMEM)] * 6,
        out_specs=(pl.BlockSpec(memory_space=pltpu.VMEM),) * 3,
        scratch_shapes=[
            pltpu.VMEM((1, TILES), jnp.int32),
            pltpu.SMEM((1, TILES), jnp.int32),
            pltpu.VMEM((TILES, LANES), F32),
            pltpu.VMEM((SLOTS, LANES), F32),
            pltpu.SemaphoreType.DMA,
        ],
        name="prep",
    )(owner, block, step, obs, direction, footprints)


def main_kernel(
    sol_ref,
    res_ref,
    dir_ref,
    noise_ref,
    owner_ref,
    obs_ref,
    lane_ref,
    values_ref,
    meta_ref,
    cov_hbm,
    time_ref,
    new_sol_ref,
    new_res_ref,
    new_dir_ref,
    cov,
    got,
    got_meta,
    acc,
    flux,
    mixed,
    mix_a,
    mix_b,
    time_a,
    time_b,
    part_a,
    part_b,
    in_a,
    in_b,
    smooth,
    dots,
    dots_back,
    sums,
    sums_in,
    cov_sem,
    tile_send,
    tile_recv,
    meta_send,
    meta_recv,
    z_send,
    z_recv,
    time_send,
    time_recv,
    ag_send,
    ag_recv,
    rs_send,
    rs_recv,
    back_send,
    back_recv,
    sum_send,
    sum_recv,
):
    cell, tm = lax.axis_index("cell"), lax.axis_index("tm")
    me = cell * 16 + tm
    z, core = cell // 2, cell % 2
    y, x = tm // 4, tm % 4

    def remote(src, dst, send, recv, to_cell, to_tm):
        return pltpu.make_async_remote_copy(
            src_ref=src,
            dst_ref=dst,
            send_sem=send,
            recv_sem=recv,
            device_id=(to_cell, to_tm),
            device_id_type=MESH,
        )

    def arrived(ref, sem):
        pltpu.make_async_copy(ref, ref, sem).wait()

    for k in range(8):
        rows = pl.ds(k * 144, 144)
        pltpu.make_async_copy(cov_hbm.at[rows], cov.at[rows], cov_sem).start()

    def send_tiles(k, _):
        peer = (me + k) % DEV
        remote(
            values_ref.at[peer], got.at[me], tile_send, tile_recv.at[cell], peer // 16, peer % 16
        ).start()
        remote(
            meta_ref.at[peer],
            got_meta.at[me],
            meta_send,
            meta_recv.at[cell],
            peer // 16,
            peer % 16,
        ).start()
        return 0

    lax.fori_loop(1, DEV, send_tiles, 0)
    pltpu.make_async_copy(values_ref.at[me], got.at[me], tile_recv.at[cell]).start()
    pltpu.make_async_copy(meta_ref.at[me], got_meta.at[me], meta_recv.at[cell]).start()

    def x_at(k):
        return (x + k) % 4

    def y_at(k):
        return (y + k) % 4

    def z_cell(k):
        return (z + k) % 4 * 2 + core

    time_sends = []
    for k in (1, 2, 3):
        peer = y_at(k)
        copy = remote(
            time_ref.at[:, pl.ds(pl.multiple_of(peer * 512, 512), 512)],
            time_a.at[y],
            time_send.at[k - 1],
            time_recv.at[k - 1],
            cell,
            peer * 4 + x,
        )
        copy.start()
        time_sends.append(copy)
        peer = x_at(k)
        for other in range(4):
            copy = remote(
                time_ref.at[:, pl.ds(pl.multiple_of((other * 4 + peer) * 128, 128), 128)],
                time_b.at[x, :, pl.ds(other * 128, 128)],
                time_send.at[3 * k + other + (k - 1)],
                time_recv.at[3 * k + other + (k - 1)],
                cell,
                y * 4 + peer,
            )
            copy.start()
            time_sends.append(copy)
    time_a[y] = time_ref[:, pl.ds(pl.multiple_of(y * 512, 512), 512)]
    for other in range(4):
        time_b[x, :, other * 128 : other * 128 + 128] = time_ref[
            :, pl.ds(pl.multiple_of((other * 4 + x) * 128, 128), 128)
        ]

    acc[...] = jnp.zeros_like(acc)
    row_of = sub_iota(LANES, LANES).astype(F32)

    def load_meta(group):
        rows = got_meta[pl.ds(group * 16, 16)]
        return jnp.sum(rows.reshape(4, 4, 2, LANES), axis=1)

    def add_group(k, _):
        group = (cell + k) % 8
        arrived(got.at[pl.ds(group * 16, 16)], tile_recv.at[group])
        arrived(got_meta.at[pl.ds(group * 16, 16)], meta_recv.at[group])
        meta = load_meta(group)
        tiles = got[pl.ds(group * 16, 16)].reshape(512, LANES)
        for b in range(BLOCKS):
            hot = jnp.concatenate(
                [
                    jnp.where(row_of + b * 128.0 == meta[q, 1:2, :], meta[q, 0:1, :], 0.0).astype(
                        BF16
                    )
                    for q in range(4)
                ],
                axis=1,
            )
            acc[b * 128 : b * 128 + 128, :] += mul(hot, tiles)
        return 0

    lax.fori_loop(0, 8, add_group, 0)
    for b in range(BLOCKS):
        flux[cell, :, b * 128 : b * 128 + 128] = acc[b * 128 : b * 128 + 128, :].astype(BF16)

    partner = z * 2 + 1 - core
    up, down, far = z_cell(1), z_cell(3), z_cell(2)
    low, high = pl.ds(0, 64), pl.ds(64, 64)
    z_copies = []

    def z_go(block, rows, to_cell, at):
        ref = flux.at[block, rows]
        copy = remote(ref, ref, z_send.at[at], z_recv.at[at], to_cell, tm)
        copy.start()
        z_copies.append(copy)

    def z_wait(block, rows, at):
        arrived(flux.at[block, rows], z_recv.at[at])

    full = pl.ds(0, 128)
    z_go(cell, full, up, 0)
    z_go(cell, full, down, 1)
    z_go(cell, full, partner, 2)

    arrived(cov, cov_sem)

    def other_core(c):
        return c // 2 * 2 + 1 - c % 2

    def mix(block, first=False):
        cols = pl.ds(pl.multiple_of(block * ROWS, 128), ROWS)
        product = mul(cov[:, cols], flux[block], NT)
        if first:
            mixed[...] = product
        else:
            mixed[...] += product

    z_wait(down, full, 0)
    z_go(down, low, up, 3)
    z_go(down, full, partner, 4)
    z_wait(up, full, 1)
    z_go(up, high, down, 5)
    z_go(up, full, partner, 6)
    mix(cell, True)
    z_wait(far, low, 3)
    z_go(far, low, partner, 7)
    z_wait(far, high, 5)
    z_go(far, high, partner, 8)
    mix(down)
    mix(up)
    z_wait(other_core(cell), full, 2)
    mix(other_core(cell))
    z_wait(other_core(down), full, 4)
    mix(other_core(down))
    z_wait(other_core(up), full, 6)
    mix(other_core(up))
    mix(far)
    z_wait(other_core(far), low, 7)
    z_wait(other_core(far), high, 8)
    mix(other_core(far))

    mix_a[:, pl.ds(pl.multiple_of(x * 128, 128), 128)] = mixed[:HALF, :].astype(BF16)
    mix_b[:, pl.ds(pl.multiple_of(y * 128, 128), 128)] = mixed[HALF:, :].astype(BF16)
    ag_copies = []

    def ag_go(buf, at_lane, rows, to_tm, at):
        ref = buf.at[rows, pl.ds(pl.multiple_of(at_lane * 128, 128), 128)]
        copy = remote(ref, ref, ag_send.at[at], ag_recv.at[at], cell, to_tm)
        copy.start()
        ag_copies.append(copy)

    def ag_wait(buf, at_lane, rows, at):
        arrived(buf.at[rows, pl.ds(pl.multiple_of(at_lane * 128, 128), 128)], ag_recv.at[at])

    every, first, second = pl.ds(0, HALF), pl.ds(0, QUARTER), pl.ds(QUARTER, QUARTER)
    x_up, x_down = y * 4 + x_at(1), y * 4 + x_at(3)
    y_up, y_down = y_at(1) * 4 + x, y_at(3) * 4 + x
    ag_go(mix_a, x, every, x_up, 0)
    ag_go(mix_a, x, every, x_down, 1)
    ag_go(mix_b, y, every, y_up, 2)
    ag_go(mix_b, y, every, y_down, 3)
    ag_wait(mix_a, x_at(3), every, 0)
    ag_go(mix_a, x_at(3), first, x_up, 4)
    ag_wait(mix_a, x_at(1), every, 1)
    ag_go(mix_a, x_at(1), second, x_down, 5)
    ag_wait(mix_b, y_at(3), every, 2)
    ag_go(mix_b, y_at(3), first, y_up, 6)
    ag_wait(mix_b, y_at(1), every, 3)
    ag_go(mix_b, y_at(1), second, y_down, 7)
    for k in (1, 2, 3):
        arrived(time_a.at[y_at(4 - k)], time_recv.at[k - 1])
        for other in range(4):
            arrived(
                time_b.at[x_at(4 - k), :, pl.ds(other * 128, 128)],
                time_recv.at[3 * k + other + (k - 1)],
            )
    ag_wait(mix_a, x_at(2), first, 4)
    ag_wait(mix_a, x_at(2), second, 5)
    rs_copies = []
    for k in (2, 1, 3):
        peer = y_at(k)
        part_a[k - 1] = mul(mix_a[...], time_a[peer], NT).astype(BF16)
        copy = remote(
            part_a.at[k - 1],
            in_a.at[k - 1],
            rs_send.at[k - 1],
            rs_recv.at[k - 1],
            cell,
            peer * 4 + x,
        )
        copy.start()
        rs_copies.append(copy)
    ag_wait(mix_b, y_at(2), first, 6)
    ag_wait(mix_b, y_at(2), second, 7)
    for k in (2, 1, 3):
        peer = x_at(k)
        part_b[k - 1] = mul(mix_b[...], time_b[peer], NT).astype(BF16)
        copy = remote(
            part_b.at[k - 1],
            in_b.at[k - 1],
            rs_send.at[k + 2],
            rs_recv.at[k + 2],
            cell,
            y * 4 + peer,
        )
        copy.start()
        rs_copies.append(copy)
    mixed[:HALF, :] = mul(mix_a[...], time_a[y], NT)
    mixed[HALF:, :] = mul(mix_b[...], time_b[x], NT)
    for k in (1, 3, 2):
        arrived(in_a.at[k - 1], rs_recv.at[k - 1])
        mixed[:HALF, :] += in_a[k - 1].astype(F32)
        arrived(in_b.at[k - 1], rs_recv.at[k + 2])
        mixed[HALF:, :] += in_b[k - 1].astype(F32)
    for b in range(BLOCKS):
        smooth[b] = mixed[b * 128 : b * 128 + 128, :].T.astype(BF16)

    def dot_group(k, _):
        group = (cell + k) % 8
        meta = load_meta(group)
        tiles = got[pl.ds(group * 16, 16)].reshape(512, LANES)
        picked = [jnp.zeros((LANES, LANES), F32) for _ in range(4)]
        for b in range(BLOCKS):
            product = mul(smooth[b], tiles, NT)
            for q in range(4):
                picked[q] += jnp.where(
                    row_of + b * 128.0 == meta[q, 1:2, :],
                    product[:, q * 128 : q * 128 + 128],
                    0.0,
                )
        for q in range(4):
            dots[group * 4 + q] = jnp.sum(picked[q], axis=0, keepdims=True)
        return 0

    lax.fori_loop(0, 8, dot_group, 0)

    def send_back(k, _):
        peer = (me + k) % DEV
        remote(
            dots.at[peer // 4], dots_back.at[me], back_send, back_recv, peer // 16, peer % 16
        ).start()
        return 0

    lax.fori_loop(1, DEV, send_back, 0)
    dots_back[me] = dots[me // 4]
    owner_hot = hot_of(owner_ref[...], DEV)
    obs_hot = hot_of(obs_ref[...], OBS)
    pltpu.make_async_copy(
        dots_back.at[pl.ds(0, DEV - 1)], dots_back.at[pl.ds(0, DEV - 1)], back_recv
    ).wait()
    by_lane = mul(dots_back[:, 0, :].T, owner_hot, precision=HIGHEST)
    tile_dots = jnp.sum(
        jnp.where(sub_iota(LANES, TILES) == lane_ref[...], by_lane, 0.0), axis=0, keepdims=True
    )
    direction, residual = dir_ref[...], res_ref[...]
    applied = mul(jnp.broadcast_to(tile_dots, (8, TILES)), obs_hot, NT, HIGHEST)[0:1, :]
    applied = applied + noise_ref[...] * direction

    lanes = lax.broadcasted_iota(jnp.int32, (1, LANES), 1)
    row = jnp.zeros((1, LANES), F32)
    for at, value in enumerate(
        (residual * residual, direction * applied, residual * applied, applied * applied)
    ):
        row = jnp.where(lanes == at, jnp.sum(value, axis=1, keepdims=True), row)
    sums[...] = row

    def send_sums(k, _):
        peer = (me + k) % DEV
        remote(sums, sums_in.at[me], sum_send, sum_recv, peer // 16, peer % 16).start()
        return 0

    lax.fori_loop(1, DEV, send_sums, 0)
    sums_in[me] = row
    pltpu.make_async_copy(
        sums_in.at[pl.ds(0, DEV - 1)], sums_in.at[pl.ds(0, DEV - 1)], sum_recv
    ).wait()
    total = jnp.sum(sums_in[...], axis=0)

    def total_of(at):
        return jnp.sum(jnp.where(lanes == at, total, 0.0), axis=1, keepdims=True)

    norm_now, curvature, cross_term, image_norm = (total_of(at) for at in range(4))
    step_size = norm_now / curvature
    new_res = residual - step_size * applied
    norm_next = norm_now - 2.0 * step_size * cross_term + step_size * step_size * image_norm
    new_sol_ref[...] = sol_ref[...] + step_size * direction
    new_res_ref[...] = new_res
    new_dir_ref[...] = new_res + norm_next / norm_now * direction

    arrived(values_ref.at[pl.ds(0, DEV - 1)], tile_send)
    arrived(meta_ref.at[pl.ds(0, DEV - 1)], meta_send)
    for copy in time_sends + z_copies + ag_copies + rs_copies:
        copy.wait_send()
    arrived(dots_back.at[pl.ds(0, DEV - 1)], back_send)
    arrived(sums_in.at[pl.ds(0, DEV - 1)], sum_send)


def whole(*operands):
    vmem = pl.BlockSpec(memory_space=pltpu.VMEM)
    dma = pltpu.SemaphoreType.DMA
    row = jax.ShapeDtypeStruct((1, OBS), F32)
    return pl.pallas_call(
        main_kernel,
        out_shape=(row, row, row),
        in_specs=[vmem] * 9 + [pl.BlockSpec(memory_space=pl.ANY), vmem],
        out_specs=(vmem, vmem, vmem),
        scratch_shapes=[
            pltpu.VMEM((ROWS, 8 * ROWS), BF16),
            pltpu.VMEM((DEV, CAP, LANES), BF16),
            pltpu.VMEM((DEV, 2, LANES), F32),
            pltpu.VMEM((ROWS, LANES), F32),
            pltpu.VMEM((8, LANES, ROWS), BF16),
            pltpu.VMEM((ROWS, LANES), F32),
            pltpu.VMEM((HALF, 512), BF16),
            pltpu.VMEM((HALF, 512), BF16),
            pltpu.VMEM((4, LANES, 512), BF16),
            pltpu.VMEM((4, LANES, 512), BF16),
            pltpu.VMEM((3, HALF, LANES), BF16),
            pltpu.VMEM((3, HALF, LANES), BF16),
            pltpu.VMEM((3, HALF, LANES), BF16),
            pltpu.VMEM((3, HALF, LANES), BF16),
            pltpu.VMEM((BLOCKS, LANES, LANES), BF16),
            pltpu.VMEM((DEV // 4, 1, LANES), F32),
            pltpu.VMEM((DEV, 1, LANES), F32),
            pltpu.VMEM((1, LANES), F32),
            pltpu.VMEM((DEV, 1, LANES), F32),
            dma,
            dma,
            dma((8,)),
            dma,
            dma((8,)),
            dma((9,)),
            dma((9,)),
            dma((15,)),
            dma((15,)),
            dma((8,)),
            dma((8,)),
            dma((6,)),
            dma((6,)),
            dma,
            dma,
            dma,
            dma,
        ],
        compiler_params=pltpu.CompilerParams(has_side_effects=True, vmem_limit_bytes=60 * 2**20),
        name="whole",
    )(*operands)


def local(
    solution,
    residual,
    direction,
    noise_var,
    footprints,
    tile_owner,
    tile_block,
    tile_step,
    tile_obs,
    cell_cov,
    time_cov,
):
    row = functools.partial(jnp.reshape, shape=(1, OBS))
    tile_row = functools.partial(jnp.reshape, shape=(1, TILES))
    owner, obs = tile_row(tile_owner), tile_row(tile_obs)
    values, meta, lane = prep(
        owner, tile_row(tile_block), tile_row(tile_step), obs, row(direction), footprints
    )
    outs = whole(
        row(solution),
        row(residual),
        row(direction),
        row(noise_var),
        owner,
        obs,
        lane,
        values.reshape(DEV, CAP, LANES),
        meta,
        cell_cov,
        time_cov,
    )
    return tuple(out.reshape(OBS) for out in outs)


def solution(mesh):
    both = P(CELL_TM)
    in_specs = (both,) * 4 + (P(CELL_TM, None),) * 2 + (both,) * 3
    in_specs += (P("cell", None), P("tm", None))
    return jax.shard_map(
        local, mesh=mesh, in_specs=in_specs, out_specs=(both,) * 3, check_vma=False
    )
```

time: 306 us -> 112 us (0.37); the launches traced: 303 us -> 112 us
  Pallas kernels: 0 us -> 108 us
  waiting for transfers between devices: 80.2 us -> 0 us
  blocking collectives: 61.1 us -> 0 us
  local copies, waits for them, and re-layouts: 59.3 us -> 3.71 us
  starting transfers between devices: 36.1 us -> 0 us
  other arithmetic: 30.3 us -> 0 us
  between operations: 18.3 us -> 0.65 us
  matrix products: 17.3 us -> 0 us
    pallas_call x0 -> x2, Pallas kernels: none -> 108 us  [the longest x1 101 us: whole(): pl.pallas_call(main_kernel, out_shape=(row, row, row), in_specs=[vmem] *...]
    all_gather x1 -> x0, waiting for transfers between devices: 50.4 us -> none  [local(): lax.all_gather(mixed_cells, TM, axis=1, tiled=True)]
    all_to_all x4 -> x0, starting transfers between devices: 35.9 us -> none  [the longest x1 11.5 us: local(): lax.all_to_all(send_dir.reshape(devices, capacity), CELL_TM, split_axis=0...]
    all_to_all x1 -> x0, blocking collectives: 33.4 us -> none  [from_everyone(): lax.all_to_all(jnp.broadcast_to(value[None], (peers, *value.shape)), axis...]
    scatter x3 -> x0, local copies, waits for them, and re-layouts: 29.8 us -> none  [the longest x1 14.6 us: local(): jnp.zeros((slot_total,), jnp.bfloat16).at[slot_index].set(dir_tile)]
    all_to_all x4 -> x0, waiting for transfers between devices: 29.8 us -> none  [the longest x1 16.9 us: local(): lax.all_to_all(send_values.reshape(devices, capacity, block_len), CELL_TM...]
    psum x4 -> x0, blocking collectives: 27.7 us -> none  [over_axes(): return functools.reduce(lax.psum, axes, value)]
    gather x2 -> x0, local copies, waits for them, and re-layouts: 23.9 us -> none  [the longest x1 12.1 us: local(): smoothed[got_place].astype(jnp.float32)]
  transfers between devices with their start and end apart: 5 -> 0, of which waited for: 5 -> 0; matrix products, arithmetic and copies ran while one was open for 6% -> 0% of each run, Pallas kernels for 0% -> 0%
where the time goes in v1:
time: 112 us
  Pallas kernels  108 us (96%)
  local copies, waits for them, and re-layouts  3.71 us (3%)
    pallas_call x1, Pallas kernels, whole(): pl.pallas_call(main_kernel, out_shape=(row, row, row), in_specs=[vmem] *...  101 us
    pallas_call x1, Pallas kernels, prep(): pl.pallas_call(prep_kernel, out_shape=(jax.ShapeDtypeStruct((SLOTS, LANES...  6.03 us
    unnamed x3, local copies, waits for them, and re-layouts  3.71 us

profile of v1, /device:TPU:1, one launch (start us, length us, event | category | flops | bytes accessed | tf_op | source)
XLA Modules:
  0.0 111.9 jit_solution(2222473004329890199)
XLA Ops:
  0.6 6.0 %prep.1 = (bf16[4096,128]{1,0:T(8,128)(2,1)}, f32[128,2,128]{2,1,0:T(2,128)}, s32[1,2048]{1,0:T(1,128)}) custom-call(s32[1,2048]{1,0:T(1,128)} %bitcast.13, s32[1,2048]{1,0:T(1,128)} %bitcast.17, s32[1,2048]{1,0:T(1,128)} %bitcast.18, s32[1,2048]{1,0:T(1,128)} %bitcast.15, f32[1,256]{1,0:T(1,128)} %bitcast.19, bf16[2048,128]{1,0:T(8,128)(2,1)} %foot_ref.1), custom_call_target="tpu_custom_call" | custom-call | tf_op jit(solution)/shard_map/prep/pallas_call | solution.py:103
  6.7 101.5 %whole.1 = (f32[1,256]{1,0:T(1,128)}, f32[1,256]{1,0:T(1,128)}, f32[1,256]{1,0:T(1,128)}) custom-call(f32[1,256]{1,0:T(1,128)} %bitcast.21, f32[1,256]{1,0:T(1,128)} %bitcast.22, f32[1,256]{1,0:T(1,128)} %bitcast.20, f32[1,256]{1,0:T(1,128)} %bitcast.23, s32[1,2048]{1,0:T(1,128)} %bitcast.14, s32[1,2048]{1,0:T(1,128)} %bitcast.16, ...), custom_call_target="tpu_custom_call" | custom-call | tf_op jit(solution)/shard_map/whole/pallas_call | solution.py:502
  108.2 1.2 %copy.17 = f32[256]{0:T(256)} copy(f32[256]{0:T(256)} %bitcast.26) | data formatting | bytes 2048
  109.4 1.2 %copy.18 = f32[256]{0:T(256)} copy(f32[256]{0:T(256)} %bitcast.25) | data formatting | bytes 2048
  110.6 1.2 %copy.19 = f32[256]{0:T(256)} copy(f32[256]{0:T(256)} %bitcast.24) | data formatting | bytes 2048

commit v2 on v1

v2 whole, which is shorter than its diff:
```python
import functools

import jax
import jax.numpy as jnp
from jax import lax
from jax.experimental import pallas as pl
from jax.experimental.pallas import tpu as pltpu
from jax.sharding import PartitionSpec as P

MESH = pl.DeviceIdType.MESH
CELL_TM = ("cell", "tm")
NN = (((1,), (0,)), ((), ()))
NT = (((1,), (1,)), ((), ()))
DEV = 128
CAP = 32
LANES = 128
OBS = 256
TILES = 2048
SLOTS = DEV * CAP
ROWS = 1152
BLOCKS = 9
HALF = ROWS // 2
QUARTER = ROWS // 4
BF16 = jnp.bfloat16
F32 = jnp.float32


def mul(a, b, dims=NN):
    return lax.dot_general(a, b, dims, preferred_element_type=F32)


def sub_iota(rows, cols):
    return lax.broadcasted_iota(jnp.int32, (rows, cols), 0)


def hot_of(index, rows):
    return jnp.where(sub_iota(rows, index.shape[1]) == index, 1.0, 0.0)


def split3(value):
    high = value.astype(BF16)
    rest = value - high.astype(F32)
    middle = rest.astype(BF16)
    return high, middle, (rest - middle.astype(F32)).astype(BF16)


def main_kernel(
    res_ref,
    dir_ref,
    noise_ref,
    owner_ref,
    block_ref,
    step_ref,
    obs_ref,
    foot_ref,
    cov_hbm,
    time_ref,
    out_ref,
    rank_row,
    index_vmem,
    index_smem,
    wide,
    slots,
    values,
    meta,
    cov,
    got,
    got_meta,
    acc,
    flux,
    mixed,
    mix_a,
    mix_b,
    time_a,
    time_b,
    part_a,
    part_b,
    in_a,
    in_b,
    smooth,
    dots,
    dots_back,
    by_rank,
    sums,
    sums_in,
    index_sem,
    cov_sem,
    tile_send,
    tile_recv,
    meta_send,
    meta_recv,
    z_send,
    z_recv,
    time_send,
    time_recv,
    ag_send,
    ag_recv,
    rs_send,
    rs_recv,
    back_send,
    back_recv,
    sum_send,
    sum_recv,
):
    cell, tm = lax.axis_index("cell"), lax.axis_index("tm")
    me = cell * 16 + tm
    z, core = cell // 2, cell % 2
    y, x = tm // 4, tm % 4
    xs = [(x + k) % 4 for k in range(4)]
    ys = [(y + k) % 4 for k in range(4)]
    far_first = sorted(
        ((dy, dx) for dy in range(4) for dx in range(4)),
        key=lambda at: -(min(at[0], 4 - at[0]) + min(at[1], 4 - at[1])),
    )
    planes = [ys[dy] * 4 + xs[dx] for dy, dx in far_first]

    def x_at(k):
        return xs[k]

    def y_at(k):
        return ys[k]

    def z_cell(k):
        return (z + k) % 4 * 2 + core

    def remote(src, dst, send, recv, to_cell, to_tm):
        return pltpu.make_async_remote_copy(
            src_ref=src,
            dst_ref=dst,
            send_sem=send,
            recv_sem=recv,
            device_id=(to_cell, to_tm),
            device_id_type=MESH,
        )

    def arrived(ref, sem):
        pltpu.make_async_copy(ref, ref, sem).wait()

    def to_others(send):
        def at_cell(k, _):
            to_cell = (cell + 4 + k) % 8
            for to_tm in planes[:15]:
                send(to_cell, to_tm)

            @pl.when(k != 4)
            def _():
                send(to_cell, planes[15])

            return 0

        lax.fori_loop(0, 8, at_cell, 0)

    barrier = pltpu.get_barrier_semaphore()
    to_others(
        lambda to_cell, to_tm: pl.semaphore_signal(
            barrier, inc=1, device_id=(to_cell, to_tm), device_id_type=MESH
        )
    )
    for k in range(8):
        rows = pl.ds(k * 144, 144)
        pltpu.make_async_copy(cov_hbm.at[rows], cov.at[rows], cov_sem).start()

    width = 256
    above = jnp.where(
        sub_iota(width, width) < lax.broadcasted_iota(jnp.int32, (width, width), 1), 1.0, 0.0
    ).astype(BF16)
    carry = jnp.zeros((DEV, 1), F32)
    for at in range(0, TILES, width):
        hot = hot_of(owner_ref[:, at : at + width], DEV)
        before = mul(hot.astype(BF16), above) + carry
        rank_row[:, at : at + width] = jnp.sum(hot * before, axis=0, keepdims=True)
        carry = before[:, width - 1 : width] + hot[:, width - 1 : width]
    owner_hot = hot_of(owner_ref[...], DEV).astype(BF16)
    in_slot = sub_iota(CAP, TILES).astype(F32) == rank_row[...]
    tile = lax.broadcasted_iota(jnp.int32, (1, TILES), 1)

    def placed(*rows):
        placings = [jnp.where(in_slot, row, 0.0).astype(BF16) for row in rows]
        return mul(owner_hot, jnp.concatenate(placings, axis=0), NT)

    index = placed((tile // 256).astype(F32), (tile % 256).astype(F32))
    index = (index[:, :CAP] * 256.0 + index[:, CAP:]).astype(jnp.int32)
    index_vmem[...] = jnp.concatenate([index] * 4, axis=1)
    index_copy = pltpu.make_async_copy(index_vmem, index_smem, index_sem)
    index_copy.start()
    wide[...] = foot_ref[...].astype(F32)
    obs_hot = hot_of(obs_ref[...], OBS).astype(BF16)
    dir_tile = mul(jnp.broadcast_to(dir_ref[...], (8, OBS)).astype(BF16), obs_hot)[0:1, :]
    fields = placed(dir_tile, block_ref[...].astype(F32), step_ref[...].astype(F32)).astype(BF16)
    lane_base = x * CAP
    shift = jnp.where(
        sub_iota(CAP, LANES) + lane_base == lax.broadcasted_iota(jnp.int32, (CAP, LANES), 1),
        1.0,
        0.0,
    ).astype(BF16)
    meta[:, 0, :] = mul(fields[:, :CAP], shift)
    meta[:, 1, :] = (
        mul(fields[:, CAP : 2 * CAP], shift) * 128.0 + mul(fields[:, 2 * CAP :], shift)
    )
    index_copy.wait()

    def gather(owner, _):
        for k in range(CAP):
            at = jnp.minimum(jnp.maximum(index_smem[owner, k], 0), TILES - 1)
            slots[pl.ds(owner * CAP + k, 1), :] = wide[pl.ds(at, 1), :]
        return 0

    lax.fori_loop(0, DEV, gather, 0)
    values[...] = slots[...].reshape(DEV, CAP, LANES).astype(BF16)
    pl.semaphore_wait(barrier, DEV - 1)

    def send_tile(to_cell, to_tm):
        peer = to_cell * 16 + to_tm
        remote(
            values.at[peer], got.at[me], tile_send, tile_recv.at[cell], to_cell, to_tm
        ).start()
        remote(
            meta.at[peer], got_meta.at[me], meta_send, meta_recv.at[cell], to_cell, to_tm
        ).start()

    to_others(send_tile)
    pltpu.make_async_copy(values.at[me], got.at[me], tile_recv.at[cell]).start()
    pltpu.make_async_copy(meta.at[me], got_meta.at[me], meta_recv.at[cell]).start()

    acc[...] = jnp.zeros_like(acc)
    row_of = sub_iota(LANES, LANES).astype(F32)

    def load_meta(group):
        rows = got_meta[pl.ds(group * 16, 16)]
        return jnp.sum(rows.reshape(4, 4, 2, LANES), axis=1)

    def add_group(k, _):
        group = (cell + 12 - k) % 8
        arrived(got.at[pl.ds(group * 16, 16)], tile_recv.at[group])
        arrived(got_meta.at[pl.ds(group * 16, 16)], meta_recv.at[group])
        rows = load_meta(group)
        tiles = got[pl.ds(group * 16, 16)].reshape(512, LANES)
        for b in range(BLOCKS):
            hot = jnp.concatenate(
                [
                    jnp.where(row_of + b * 128.0 == rows[q, 1:2, :], rows[q, 0:1, :], 0.0).astype(
                        BF16
                    )
                    for q in range(4)
                ],
                axis=1,
            )
            acc[b * 128 : b * 128 + 128, :] += mul(hot, tiles)
        return 0

    lax.fori_loop(0, 8, add_group, 0)
    for b in range(BLOCKS):
        flux[cell, :, b * 128 : b * 128 + 128] = acc[b * 128 : b * 128 + 128, :].astype(BF16)

    partner = z * 2 + 1 - core
    up, down, far = z_cell(1), z_cell(3), z_cell(2)
    left, right, full = pl.ds(0, 512), pl.ds(512, ROWS - 512), pl.ds(0, ROWS)
    z_copies = []

    def z_go(block, cols, to_cell, at):
        ref = flux.at[block, :, cols]
        copy = remote(ref, ref, z_send.at[at], z_recv.at[at], to_cell, tm)
        copy.start()
        z_copies.append(copy)

    def z_wait(block, cols, at):
        arrived(flux.at[block, :, cols], z_recv.at[at])

    z_go(cell, left, up, 0)
    z_go(cell, right, down, 2)
    z_go(cell, right, up, 1)
    z_go(cell, left, down, 3)
    z_go(cell, full, partner, 4)

    time_sends = []
    for k in (1, 2, 3):
        peer = y_at(k)
        copy = remote(
            time_ref.at[:, pl.ds(pl.multiple_of(peer * 512, 512), 512)],
            time_a.at[y],
            time_send.at[k - 1],
            time_recv.at[k - 1],
            cell,
            peer * 4 + x,
        )
        copy.start()
        time_sends.append(copy)
        peer = x_at(k)
        for other in range(4):
            copy = remote(
                time_ref.at[:, pl.ds(pl.multiple_of((other * 4 + peer) * 128, 128), 128)],
                time_b.at[x, :, pl.ds(other * 128, 128)],
                time_send.at[3 * k + other + (k - 1)],
                time_recv.at[3 * k + other + (k - 1)],
                cell,
                y * 4 + peer,
            )
            copy.start()
            time_sends.append(copy)
    time_a[y] = time_ref[:, pl.ds(pl.multiple_of(y * 512, 512), 512)]
    for other in range(4):
        time_b[x, :, other * 128 : other * 128 + 128] = time_ref[
            :, pl.ds(pl.multiple_of((other * 4 + x) * 128, 128), 128)
        ]

    arrived(cov, cov_sem)

    def other_core(c):
        return c // 2 * 2 + 1 - c % 2

    def mix(block, first=False):
        cols = pl.ds(pl.multiple_of(block * ROWS, 128), ROWS)
        product = mul(cov[:, cols], flux[block], NT)
        if first:
            mixed[...] = product
        else:
            mixed[...] += product

    mix(cell, True)
    z_wait(down, left, 0)
    z_go(down, left, up, 5)
    z_go(down, left, partner, 7)
    z_wait(up, right, 2)
    z_go(up, right, down, 6)
    z_go(up, right, partner, 8)
    z_wait(other_core(cell), full, 4)
    mix(other_core(cell))
    z_wait(down, right, 1)
    z_go(down, right, partner, 9)
    z_wait(up, left, 3)
    z_go(up, left, partner, 10)
    mix(down)
    mix(up)
    z_wait(other_core(down), left, 7)
    z_wait(other_core(down), right, 9)
    mix(other_core(down))
    z_wait(other_core(up), right, 8)
    z_wait(other_core(up), left, 10)
    mix(other_core(up))
    z_wait(far, left, 5)
    z_go(far, left, partner, 11)
    z_wait(far, right, 6)
    z_go(far, right, partner, 12)
    mix(far)
    z_wait(other_core(far), left, 11)
    z_wait(other_core(far), right, 12)
    mix(other_core(far))

    mix_a[:, pl.ds(pl.multiple_of(x * 128, 128), 128)] = mixed[:HALF, :].astype(BF16)
    mix_b[:, pl.ds(pl.multiple_of(y * 128, 128), 128)] = mixed[HALF:, :].astype(BF16)
    ag_copies = []

    def ag_go(buf, at_lane, rows, to_tm, at):
        ref = buf.at[rows, pl.ds(pl.multiple_of(at_lane * 128, 128), 128)]
        copy = remote(ref, ref, ag_send.at[at], ag_recv.at[at], cell, to_tm)
        copy.start()
        ag_copies.append(copy)

    def ag_wait(buf, at_lane, rows, at):
        arrived(buf.at[rows, pl.ds(pl.multiple_of(at_lane * 128, 128), 128)], ag_recv.at[at])

    first, second = pl.ds(0, QUARTER), pl.ds(QUARTER, QUARTER)
    x_up, x_down = y * 4 + x_at(1), y * 4 + x_at(3)
    y_up, y_down = y_at(1) * 4 + x, y_at(3) * 4 + x
    ag_go(mix_a, x, first, x_up, 0)
    ag_go(mix_a, x, second, x_down, 1)
    ag_go(mix_b, y, first, y_up, 2)
    ag_go(mix_b, y, second, y_down, 3)
    ag_go(mix_a, x, second, x_up, 4)
    ag_go(mix_a, x, first, x_down, 5)
    ag_go(mix_b, y, second, y_up, 6)
    ag_go(mix_b, y, first, y_down, 7)
    ag_wait(mix_a, x_at(3), first, 0)
    ag_go(mix_a, x_at(3), first, x_up, 8)
    ag_wait(mix_a, x_at(1), second, 1)
    ag_go(mix_a, x_at(1), second, x_down, 9)
    ag_wait(mix_b, y_at(3), first, 2)
    ag_go(mix_b, y_at(3), first, y_up, 10)
    ag_wait(mix_b, y_at(1), second, 3)
    ag_go(mix_b, y_at(1), second, y_down, 11)
    for k in (1, 2, 3):
        arrived(time_a.at[y_at(4 - k)], time_recv.at[k - 1])
        for other in range(4):
            arrived(
                time_b.at[x_at(4 - k), :, pl.ds(other * 128, 128)],
                time_recv.at[3 * k + other + (k - 1)],
            )
    ag_wait(mix_a, x_at(3), second, 4)
    ag_wait(mix_a, x_at(1), first, 5)
    ag_wait(mix_b, y_at(3), second, 6)
    ag_wait(mix_b, y_at(1), first, 7)
    ag_wait(mix_a, x_at(2), first, 8)
    ag_wait(mix_a, x_at(2), second, 9)
    rs_copies = []
    for k in (2, 1, 3):
        peer = y_at(k)
        part_a[k - 1] = mul(mix_a[...], time_a[peer], NT).astype(BF16)
        copy = remote(
            part_a.at[k - 1],
            in_a.at[k - 1],
            rs_send.at[k - 1],
            rs_recv.at[k - 1],
            cell,
            peer * 4 + x,
        )
        copy.start()
        rs_copies.append(copy)
        if k == 2:
            ag_wait(mix_b, y_at(2), first, 10)
            ag_wait(mix_b, y_at(2), second, 11)
        peer = x_at(k)
        part_b[k - 1] = mul(mix_b[...], time_b[peer], NT).astype(BF16)
        copy = remote(
            part_b.at[k - 1],
            in_b.at[k - 1],
            rs_send.at[k + 2],
            rs_recv.at[k + 2],
            cell,
            y * 4 + peer,
        )
        copy.start()
        rs_copies.append(copy)
    mixed[:HALF, :] = mul(mix_a[...], time_a[y], NT)
    mixed[HALF:, :] = mul(mix_b[...], time_b[x], NT)
    for k in (1, 3, 2):
        arrived(in_a.at[k - 1], rs_recv.at[k - 1])
        mixed[:HALF, :] += in_a[k - 1].astype(F32)
        arrived(in_b.at[k - 1], rs_recv.at[k + 2])
        mixed[HALF:, :] += in_b[k - 1].astype(F32)
    for b in range(BLOCKS):
        smooth[b] = mixed[b * 128 : b * 128 + 128, :].T.astype(BF16)

    def dot_group(k, _):
        group = (cell + 4 + k) % 8
        rows = load_meta(group)
        tiles = got[pl.ds(group * 16, 16)].reshape(512, LANES)
        picked = [jnp.zeros((LANES, LANES), F32) for _ in range(4)]
        for b in range(BLOCKS):
            product = mul(smooth[b], tiles, NT)
            for q in range(4):
                picked[q] += jnp.where(
                    row_of + b * 128.0 == rows[q, 1:2, :],
                    product[:, q * 128 : q * 128 + 128],
                    0.0,
                )
        for q in range(4):
            dots[group * 4 + q] = jnp.sum(picked[q], axis=0, keepdims=True)

        def send_dots(to_tm):
            remote(
                dots.at[group * 4 + to_tm // 4],
                dots_back.at[me],
                back_send,
                back_recv,
                group,
                to_tm,
            ).start()

        for to_tm in planes[:15]:
            send_dots(to_tm)

        @pl.when(k != 4)
        def _():
            send_dots(planes[15])

        return 0

    lax.fori_loop(0, 8, dot_group, 0)
    dots_back[me] = dots[me // 4]
    owner_hot = hot_of(owner_ref[...], DEV).astype(BF16)
    obs_hot = hot_of(obs_ref[...], OBS).astype(BF16)
    in_slot = sub_iota(CAP, TILES).astype(F32) == rank_row[...]
    arrived(dots_back.at[pl.ds(0, DEV - 1)], back_recv)
    by_rank[...] = dots_back[:, 0, :].T
    own = jnp.concatenate(split3(by_rank[pl.ds(pl.multiple_of(lane_base, CAP), CAP), :]), axis=0)
    parts = mul(own, owner_hot)
    tile_dots = jnp.sum(
        jnp.where(in_slot, parts[:CAP] + parts[CAP : 2 * CAP] + parts[2 * CAP :], 0.0),
        axis=0,
        keepdims=True,
    )
    high, middle, low = split3(tile_dots)
    three = jnp.concatenate(
        [high.astype(F32), middle.astype(F32), low.astype(F32), jnp.zeros((5, TILES), F32)], axis=0
    ).astype(BF16)
    direction, residual = dir_ref[...], res_ref[...]
    applied = jnp.sum(mul(three, obs_hot, NT), axis=0, keepdims=True)
    applied = applied + noise_ref[...] * direction

    lanes = lax.broadcasted_iota(jnp.int32, (1, LANES), 1)
    row = jnp.zeros((1, LANES), F32)
    for at, value in enumerate(
        (residual * residual, direction * applied, residual * applied, applied * applied)
    ):
        row = jnp.where(lanes == at, jnp.sum(value, axis=1, keepdims=True), row)
    sums[...] = row
    to_others(
        lambda to_cell, to_tm: remote(
            sums, sums_in.at[me], sum_send, sum_recv, to_cell, to_tm
        ).start()
    )
    sums_in[me] = row
    arrived(sums_in.at[pl.ds(0, DEV - 1)], sum_recv)
    total = jnp.sum(sums_in[...], axis=0)

    def total_of(at):
        return jnp.sum(jnp.where(lanes == at, total, 0.0), axis=1, keepdims=True)

    norm_now, curvature, cross_term, image_norm = (total_of(at) for at in range(4))
    step_size = norm_now / curvature
    norm_next = norm_now - 2.0 * step_size * cross_term + step_size * step_size * image_norm
    out_ref[0:1, :] = applied
    out_ref[1:2, :] = jnp.broadcast_to(step_size, (1, OBS))
    out_ref[2:3, :] = jnp.broadcast_to(norm_next / norm_now, (1, OBS))

    arrived(values.at[pl.ds(0, DEV - 1)], tile_send)
    arrived(meta.at[pl.ds(0, DEV - 1)], meta_send)
    for copy in time_sends + z_copies + ag_copies + rs_copies:
        copy.wait_send()
    arrived(dots_back.at[pl.ds(0, DEV - 1)], back_send)
    arrived(sums_in.at[pl.ds(0, DEV - 1)], sum_send)


def whole(*operands):
    vmem = pl.BlockSpec(memory_space=pltpu.VMEM)
    dma = pltpu.SemaphoreType.DMA
    return pl.pallas_call(
        main_kernel,
        out_shape=jax.ShapeDtypeStruct((3, OBS), F32),
        in_specs=[vmem] * 8 + [pl.BlockSpec(memory_space=pl.ANY), vmem],
        out_specs=vmem,
        scratch_shapes=[
            pltpu.VMEM((1, TILES), F32),
            pltpu.VMEM((DEV, LANES), jnp.int32),
            pltpu.SMEM((DEV, LANES), jnp.int32),
            pltpu.VMEM((TILES, LANES), F32),
            pltpu.VMEM((SLOTS, LANES), F32),
            pltpu.VMEM((DEV, CAP, LANES), BF16),
            pltpu.VMEM((DEV, 2, LANES), F32),
            pltpu.VMEM((ROWS, 8 * ROWS), BF16),
            pltpu.VMEM((DEV, CAP, LANES), BF16),
            pltpu.VMEM((DEV, 2, LANES), F32),
            pltpu.VMEM((ROWS, LANES), F32),
            pltpu.VMEM((8, LANES, ROWS), BF16),
            pltpu.VMEM((ROWS, LANES), F32),
            pltpu.VMEM((HALF, 512), BF16),
            pltpu.VMEM((HALF, 512), BF16),
            pltpu.VMEM((4, LANES, 512), BF16),
            pltpu.VMEM((4, LANES, 512), BF16),
            pltpu.VMEM((3, HALF, LANES), BF16),
            pltpu.VMEM((3, HALF, LANES), BF16),
            pltpu.VMEM((3, HALF, LANES), BF16),
            pltpu.VMEM((3, HALF, LANES), BF16),
            pltpu.VMEM((BLOCKS, LANES, LANES), BF16),
            pltpu.VMEM((DEV // 4, 1, LANES), F32),
            pltpu.VMEM((DEV, 1, LANES), F32),
            pltpu.VMEM((LANES, DEV), F32),
            pltpu.VMEM((1, LANES), F32),
            pltpu.VMEM((DEV, 1, LANES), F32),
            dma,
            dma,
            dma,
            dma((8,)),
            dma,
            dma((8,)),
            dma((13,)),
            dma((13,)),
            dma((15,)),
            dma((15,)),
            dma((12,)),
            dma((12,)),
            dma((6,)),
            dma((6,)),
            dma,
            dma,
            dma,
            dma,
        ],
        compiler_params=pltpu.CompilerParams(
            collective_id=0, has_side_effects=True, vmem_limit_bytes=60 * 2**20
        ),
        name="whole",
    )(*operands)


def local(
    solution,
    residual,
    direction,
    noise_var,
    footprints,
    tile_owner,
    tile_block,
    tile_step,
    tile_obs,
    cell_cov,
    time_cov,
):
    row = functools.partial(jnp.reshape, shape=(1, OBS))
    tile_row = functools.partial(jnp.reshape, shape=(1, TILES))
    applied, step_size, ratio = whole(
        row(residual),
        row(direction),
        row(noise_var),
        tile_row(tile_owner),
        tile_row(tile_block),
        tile_row(tile_step),
        tile_row(tile_obs),
        footprints,
        cell_cov,
        time_cov,
    )
    new_residual = residual - step_size * applied
    return solution + step_size * direction, new_residual, new_residual + ratio * direction


def solution(mesh):
    both = P(CELL_TM)
    in_specs = (both,) * 4 + (P(CELL_TM, None),) * 2 + (both,) * 3
    in_specs += (P("cell", None), P("tm", None))
    return jax.shard_map(
        local, mesh=mesh, in_specs=in_specs, out_specs=(both,) * 3, check_vma=False
    )
```

time: 112 us -> 92.9 us (0.83)
  Pallas kernels: 108 us -> 90.7 us
  local copies, waits for them, and re-layouts: 3.71 us -> 0.81 us
    pallas_call x2 -> x1, Pallas kernels: 108 us -> 90.7 us  [whole(): pl.pallas_call(main_kernel, out_shape=jax.ShapeDtypeStruct((3, OBS), F32)...]
    unnamed x3 -> x6, local copies, waits for them, and re-layouts: 3.71 us -> 0.01 us
where the time goes in v2:
time: 92.9 us; the launch traced here: 92.7 us
  Pallas kernels  90.7 us (98%)
    pallas_call x1, Pallas kernels, whole(): pl.pallas_call(main_kernel, out_shape=jax.ShapeDtypeStruct((3, OBS), F32)...  90.7 us

profile of v2, /device:TPU:1, one launch (start us, length us, event | category | flops | bytes accessed | tf_op | source)
XLA Modules:
  0.0 92.7 jit_solution(11685358703278995751)
XLA Ops:
  0.6 0.0 copy-start.1
  0.6 0.0 copy-start
  0.7 0.0 copy-start.2
  0.7 90.7 %whole.1 = f32[3,256]{1,0:T(4,128)} custom-call(f32[1,256]{1,0:T(1,128)} %bitcast.14, f32[1,256]{1,0:T(1,128)} %bitcast.15, f32[1,256]{1,0:T(1,128)} %bitcast.19, s32[1,2048]{1,0:T(1,128)} %bitcast.10, s32[1,2048]{1,0:T(1,128)} %bitcast.11, s32[1,2048]{1,0:T(1,128)} %bitcast.12, s32[1,2048]{1,0:T(1,128)} %bitcast.13, bf16[2048,128]{1,0:T(8,128)(2,1)} %foot_ref.1, ...), custom_call_target="tpu_custom_call" | custom-call | tf_op jit(solution)/shard_map/whole/pallas_call | solution.py:527
  91.3 0.8 fusion
  92.1 0.0 copy-done.1
  92.1 0.0 copy-done
  92.1 0.0 copy-done.2
  92.1 0.6 multiply_add_fusion
Async XLA Ops:
  0.6 91.5 %copy-start.1 = (f32[256]{0:T(256)S(1)}, f32[256]{0:T(256)}, u32[]{:S(2)}) copy-start(f32[256]{0:T(256)} %param.13) | copy-start | bytes 3076
  0.6 91.5 %copy-start = (f32[256]{0:T(256)S(1)}, f32[256]{0:T(256)}, u32[]{:S(2)}) copy-start(f32[256]{0:T(256)} %param.12) | copy-start | bytes 3076
  0.7 91.5 %copy-start.2 = (f32[256]{0:T(256)S(1)}, f32[256]{0:T(256)}, u32[]{:S(2)}) copy-start(f32[256]{0:T(256)} %param.11) | copy-start | bytes 3076

commit v3 on v2

--- a/solution.py
+++ b/solution.py
@@ -44,25 +44,80 @@
     return high, middle, (rest - middle.astype(F32)).astype(BF16)
 
 
+def prep_kernel(
+    owner_ref, block_ref, step_ref, obs_ref, dir_ref, index_ref, meta_ref, rank_ref
+):
+    width = 256
+    above = jnp.where(
+        sub_iota(width, width) < lax.broadcasted_iota(jnp.int32, (width, width), 1), 1.0, 0.0
+    ).astype(BF16)
+    carry = jnp.zeros((DEV, 1), F32)
+    for at in range(0, TILES, width):
+        hot = hot_of(owner_ref[:, at : at + width], DEV)
+        before = mul(hot.astype(BF16), above) + carry
+        rank_ref[:, at : at + width] = jnp.sum(hot * before, axis=0, keepdims=True)
+        carry = before[:, width - 1 : width] + hot[:, width - 1 : width]
+    owner_hot = hot_of(owner_ref[...], DEV).astype(BF16)
+    in_slot = sub_iota(CAP, TILES).astype(F32) == rank_ref[...]
+    tile = lax.broadcasted_iota(jnp.int32, (1, TILES), 1)
+
+    def placings(*rows):
+        return jnp.concatenate([jnp.where(in_slot, row, 0.0).astype(BF16) for row in rows], axis=0)
+
+    index = mul(placings((tile // 256).astype(F32), (tile % 256).astype(F32)), owner_hot, NT)
+    index_ref[...] = (index[:CAP] * 256.0 + index[CAP:]).astype(jnp.int32)
+    obs_hot = hot_of(obs_ref[...], OBS).astype(BF16)
+    dir_tile = mul(jnp.broadcast_to(dir_ref[...], (8, OBS)).astype(BF16), obs_hot)[0:1, :]
+    fields = mul(
+        owner_hot,
+        placings(dir_tile, block_ref[...].astype(F32), step_ref[...].astype(F32)),
+        NT,
+    ).astype(BF16)
+    lane_base = lax.axis_index("tm") % 4 * CAP
+    shift = jnp.where(
+        sub_iota(CAP, LANES) + lane_base == lax.broadcasted_iota(jnp.int32, (CAP, LANES), 1),
+        1.0,
+        0.0,
+    ).astype(BF16)
+    meta_ref[:, 0, :] = mul(fields[:, :CAP], shift)
+    meta_ref[:, 1, :] = (
+        mul(fields[:, CAP : 2 * CAP], shift) * 128.0 + mul(fields[:, 2 * CAP :], shift)
+    )
+
+
+def prep(*operands):
+    vmem = pl.BlockSpec(memory_space=pltpu.VMEM)
+    return pl.pallas_call(
+        prep_kernel,
+        out_shape=(
+            jax.ShapeDtypeStruct((CAP, DEV), jnp.int32),
+            jax.ShapeDtypeStruct((DEV, 2, LANES), F32),
+            jax.ShapeDtypeStruct((1, TILES), F32),
+        ),
+        in_specs=[vmem] * 5,
+        out_specs=(vmem,) * 3,
+        name="prep",
+    )(*operands)
+
+
 def main_kernel(
     res_ref,
     dir_ref,
     noise_ref,
     owner_ref,
-    block_ref,
-    step_ref,
     obs_ref,
+    rank_ref,
+    index_ref,
+    meta_ref,
     foot_ref,
     cov_hbm,
     time_ref,
-    out_ref,
-    rank_row,
-    index_vmem,
-    index_smem,
+    applied_ref,
+    step_ref,
+    ratio_ref,
     wide,
     slots,
     values,
-    meta,
     cov,
     got,
     got_meta,
@@ -83,7 +138,6 @@
     by_rank,
     sums,
     sums_in,
-    index_sem,
     cov_sem,
     tile_send,
     tile_recv,
@@ -160,53 +214,7 @@
         rows = pl.ds(k * 144, 144)
         pltpu.make_async_copy(cov_hbm.at[rows], cov.at[rows], cov_sem).start()
 
-    width = 256
-    above = jnp.where(
-        sub_iota(width, width) < lax.broadcasted_iota(jnp.int32, (width, width), 1), 1.0, 0.0
-    ).astype(BF16)
-    carry = jnp.zeros((DEV, 1), F32)
-    for at in range(0, TILES, width):
-        hot = hot_of(owner_ref[:, at : at + width], DEV)
-        before = mul(hot.astype(BF16), above) + carry
-        rank_row[:, at : at + width] = jnp.sum(hot * before, axis=0, keepdims=True)
-        carry = before[:, width - 1 : width] + hot[:, width - 1 : width]
-    owner_hot = hot_of(owner_ref[...], DEV).astype(BF16)
-    in_slot = sub_iota(CAP, TILES).astype(F32) == rank_row[...]
-    tile = lax.broadcasted_iota(jnp.int32, (1, TILES), 1)
-
-    def placed(*rows):
-        placings = [jnp.where(in_slot, row, 0.0).astype(BF16) for row in rows]
-        return mul(owner_hot, jnp.concatenate(placings, axis=0), NT)
-
-    index = placed((tile // 256).astype(F32), (tile % 256).astype(F32))
-    index = (index[:, :CAP] * 256.0 + index[:, CAP:]).astype(jnp.int32)
-    index_vmem[...] = jnp.concatenate([index] * 4, axis=1)
-    index_copy = pltpu.make_async_copy(index_vmem, index_smem, index_sem)
-    index_copy.start()
     wide[...] = foot_ref[...].astype(F32)
-    obs_hot = hot_of(obs_ref[...], OBS).astype(BF16)
-    dir_tile = mul(jnp.broadcast_to(dir_ref[...], (8, OBS)).astype(BF16), obs_hot)[0:1, :]
-    fields = placed(dir_tile, block_ref[...].astype(F32), step_ref[...].astype(F32)).astype(BF16)
-    lane_base = x * CAP
-    shift = jnp.where(
-        sub_iota(CAP, LANES) + lane_base == lax.broadcasted_iota(jnp.int32, (CAP, LANES), 1),
-        1.0,
-        0.0,
-    ).astype(BF16)
-    meta[:, 0, :] = mul(fields[:, :CAP], shift)
-    meta[:, 1, :] = (
-        mul(fields[:, CAP : 2 * CAP], shift) * 128.0 + mul(fields[:, 2 * CAP :], shift)
-    )
-    index_copy.wait()
-
-    def gather(owner, _):
-        for k in range(CAP):
-            at = jnp.minimum(jnp.maximum(index_smem[owner, k], 0), TILES - 1)
-            slots[pl.ds(owner * CAP + k, 1), :] = wide[pl.ds(at, 1), :]
-        return 0
-
-    lax.fori_loop(0, DEV, gather, 0)
-    values[...] = slots[...].reshape(DEV, CAP, LANES).astype(BF16)
     pl.semaphore_wait(barrier, DEV - 1)
 
     def send_tile(to_cell, to_tm):
@@ -215,12 +223,28 @@
             values.at[peer], got.at[me], tile_send, tile_recv.at[cell], to_cell, to_tm
         ).start()
         remote(
-            meta.at[peer], got_meta.at[me], meta_send, meta_recv.at[cell], to_cell, to_tm
+            meta_ref.at[peer], got_meta.at[me], meta_send, meta_recv.at[cell], to_cell, to_tm
         ).start()
 
-    to_others(send_tile)
+    def gather_and_send(k, _):
+        to_cell = (cell + 4 + k) % 8
+        for j in range(16):
+            peer = to_cell * 16 + planes[j]
+            for r in range(CAP):
+                slots[j, r : r + 1, :] = wide[pl.ds(index_ref[r, peer], 1), :]
+            values[peer] = slots[j].astype(BF16)
+            if j:
+                send_tile(to_cell, planes[j - 1])
+
+        @pl.when(k != 4)
+        def _():
+            send_tile(to_cell, planes[15])
+
+        return 0
+
+    lax.fori_loop(0, 8, gather_and_send, 0)
     pltpu.make_async_copy(values.at[me], got.at[me], tile_recv.at[cell]).start()
-    pltpu.make_async_copy(meta.at[me], got_meta.at[me], meta_recv.at[cell]).start()
+    pltpu.make_async_copy(meta_ref.at[me], got_meta.at[me], meta_recv.at[cell]).start()
 
     acc[...] = jnp.zeros_like(acc)
     row_of = sub_iota(LANES, LANES).astype(F32)
@@ -469,9 +493,10 @@
     dots_back[me] = dots[me // 4]
     owner_hot = hot_of(owner_ref[...], DEV).astype(BF16)
     obs_hot = hot_of(obs_ref[...], OBS).astype(BF16)
-    in_slot = sub_iota(CAP, TILES).astype(F32) == rank_row[...]
+    in_slot = sub_iota(CAP, TILES).astype(F32) == rank_ref[...]
     arrived(dots_back.at[pl.ds(0, DEV - 1)], back_recv)
     by_rank[...] = dots_back[:, 0, :].T
+    lane_base = x * CAP
     own = jnp.concatenate(split3(by_rank[pl.ds(pl.multiple_of(lane_base, CAP), CAP), :]), axis=0)
     parts = mul(own, owner_hot)
     tile_dots = jnp.sum(
@@ -509,12 +534,12 @@
     norm_now, curvature, cross_term, image_norm = (total_of(at) for at in range(4))
     step_size = norm_now / curvature
     norm_next = norm_now - 2.0 * step_size * cross_term + step_size * step_size * image_norm
-    out_ref[0:1, :] = applied
-    out_ref[1:2, :] = jnp.broadcast_to(step_size, (1, OBS))
-    out_ref[2:3, :] = jnp.broadcast_to(norm_next / norm_now, (1, OBS))
+    applied_ref[...] = applied
+    step_ref[...] = jnp.broadcast_to(step_size, (1, OBS))
+    ratio_ref[...] = jnp.broadcast_to(norm_next / norm_now, (1, OBS))
 
     arrived(values.at[pl.ds(0, DEV - 1)], tile_send)
-    arrived(meta.at[pl.ds(0, DEV - 1)], meta_send)
+    arrived(meta_ref.at[pl.ds(0, DEV - 1)], meta_send)
     for copy in time_sends + z_copies + ag_copies + rs_copies:
         copy.wait_send()
     arrived(dots_back.at[pl.ds(0, DEV - 1)], back_send)
@@ -524,19 +549,18 @@
 def whole(*operands):
     vmem = pl.BlockSpec(memory_space=pltpu.VMEM)
     dma = pltpu.SemaphoreType.DMA
+    row = jax.ShapeDtypeStruct((1, OBS), F32)
     return pl.pallas_call(
         main_kernel,
-        out_shape=jax.ShapeDtypeStruct((3, OBS), F32),
-        in_specs=[vmem] * 8 + [pl.BlockSpec(memory_space=pl.ANY), vmem],
-        out_specs=vmem,
+        out_shape=(row, row, row),
+        in_specs=[vmem] * 6
+        + [pl.BlockSpec(memory_space=pltpu.SMEM), vmem, vmem]
+        + [pl.BlockSpec(memory_space=pl.ANY), vmem],
+        out_specs=(vmem,) * 3,
         scratch_shapes=[
-            pltpu.VMEM((1, TILES), F32),
-            pltpu.VMEM((DEV, LANES), jnp.int32),
-            pltpu.SMEM((DEV, LANES), jnp.int32),
             pltpu.VMEM((TILES, LANES), F32),
-            pltpu.VMEM((SLOTS, LANES), F32),
+            pltpu.VMEM((16, CAP, LANES), F32),
             pltpu.VMEM((DEV, CAP, LANES), BF16),
-            pltpu.VMEM((DEV, 2, LANES), F32),
             pltpu.VMEM((ROWS, 8 * ROWS), BF16),
             pltpu.VMEM((DEV, CAP, LANES), BF16),
             pltpu.VMEM((DEV, 2, LANES), F32),
@@ -557,7 +581,6 @@
             pltpu.VMEM((LANES, DEV), F32),
             pltpu.VMEM((1, LANES), F32),
             pltpu.VMEM((DEV, 1, LANES), F32),
-            dma,
             dma,
             dma,
             dma((8,)),
@@ -598,18 +621,22 @@
 ):
     row = functools.partial(jnp.reshape, shape=(1, OBS))
     tile_row = functools.partial(jnp.reshape, shape=(1, TILES))
-    applied, step_size, ratio = whole(
+    owner, obs = tile_row(tile_owner), tile_row(tile_obs)
+    index, meta, rank = prep(owner, tile_row(tile_block), tile_row(tile_step), obs, row(direction))
+    outs = whole(
         row(residual),
         row(direction),
         row(noise_var),
-        tile_row(tile_owner),
-        tile_row(tile_block),
-        tile_row(tile_step),
-        tile_row(tile_obs),
+        owner,
+        obs,
+        rank,
+        index,
+        meta,
         footprints,
         cell_cov,
         time_cov,
     )
+    applied, step_size, ratio = (out.reshape(OBS) for out in outs)
     new_residual = residual - step_size * applied
     return solution + step_size * direction, new_residual, new_residual + ratio * direction
 

time: 92.9 us -> 88.6 us (0.954)
  Pallas kernels: 90.7 us -> 86.5 us
    pallas_call x1 -> x2, Pallas kernels: 90.7 us -> 86.5 us  [the longest x1 83.5 us: whole(): pl.pallas_call(main_kernel, out_shape=(row, row, row), in_specs=[vmem] *...]
where the time goes in v3:
time: 88.6 us; the launch traced here: 88.4 us
  Pallas kernels  86.5 us (98%)
  other arithmetic  1.25 us (1%)
    pallas_call x1, Pallas kernels, whole(): pl.pallas_call(main_kernel, out_shape=(row, row, row), in_specs=[vmem] *...  83.5 us
    pallas_call x1, Pallas kernels, prep(): pl.pallas_call(prep_kernel, out_shape=(jax.ShapeDtypeStruct((CAP, DEV), j...  2.94 us

profile of v3, /device:TPU:1, one launch (start us, length us, event | category | flops | bytes accessed | tf_op | source)
XLA Modules:
  0.0 88.4 jit_solution(13486783258922276332)
XLA Ops:
  0.6 0.0 copy-start
  0.6 0.0 copy-start.1
  0.7 0.0 copy-start.2
  0.7 2.9 %prep.1 = (s32[32,128]{1,0:T(8,128)}, f32[128,2,128]{2,1,0:T(2,128)}, f32[1,2048]{1,0:T(1,128)}) custom-call(s32[1,2048]{1,0:T(1,128)} %bitcast.10, s32[1,2048]{1,0:T(1,128)} %bitcast.16, s32[1,2048]{1,0:T(1,128)} %bitcast.17, s32[1,2048]{1,0:T(1,128)} %bitcast.12, f32[1,256]{1,0:T(1,128)} %bitcast.14), custom_call_target="tpu_custom_call" | custom-call | tf_op jit(solution)/shard_map/prep/pallas_call | solution.py:90
  3.6 83.5 %whole.1 = (f32[1,256]{1,0:T(1,128)}, f32[1,256]{1,0:T(1,128)}, f32[1,256]{1,0:T(1,128)}) custom-call(f32[1,256]{1,0:T(1,128)} %bitcast.18, f32[1,256]{1,0:T(1,128)} %bitcast.15, f32[1,256]{1,0:T(1,128)} %bitcast.19, s32[1,2048]{1,0:T(1,128)} %bitcast.11, s32[1,2048]{1,0:T(1,128)} %bitcast.13, f32[1,2048]{1,0:T(1,128)} %get-tuple-element.9.rank_ref, ...), custom_call_target="tpu_custom_call" | custom-call | tf_op jit(solution)/shard_map/whole/pallas_call | solution.py:553
  87.2 0.0 copy-done
  87.2 0.0 copy-done.1
  87.2 0.0 copy-done.2
  87.2 1.2 %multiply_add_fusion = (f32[256]{0:T(256)}, f32[256]{0:T(256)}, f32[256]{0:T(256)}) fusion(f32[256]{0:T(256)} %bitcast.22, f32[256]{0:T(256)S(1)} %copy-done, f32[256]{0:T(256)S(1)} %copy-done.1, f32[256]{0:T(256)} %bitcast.21, f32[256]{0:T(256)} %bitcast.20, f32[256]{0:T(256)S(1)} %copy-done.2), kind=kLoop, calls=%fused_computation | loop fusion | flops 1536 | bytes 9216 | tf_op jit(solution)/shard_map/add | solution.py:641
Async XLA Ops:
  0.6 86.5 %copy-start = (f32[256]{0:T(256)S(1)}, f32[256]{0:T(256)}, u32[]{:S(2)}) copy-start(f32[256]{0:T(256)} %param.13) | copy-start | bytes 3076
  0.6 86.5 %copy-start.1 = (f32[256]{0:T(256)S(1)}, f32[256]{0:T(256)}, u32[]{:S(2)}) copy-start(f32[256]{0:T(256)} %param.12) | copy-start | bytes 3076
  0.7 86.5 %copy-start.2 = (f32[256]{0:T(256)S(1)}, f32[256]{0:T(256)}, u32[]{:S(2)}) copy-start(f32[256]{0:T(256)} %param.11) | copy-start | bytes 3076

commit v4 on v3

--- a/solution.py
+++ b/solution.py
@@ -44,9 +44,12 @@
     return high, middle, (rest - middle.astype(F32)).astype(BF16)
 
 
-def prep_kernel(
-    owner_ref, block_ref, step_ref, obs_ref, dir_ref, index_ref, meta_ref, rank_ref
-):
+def placings(rank, *rows):
+    in_slot = sub_iota(CAP, TILES).astype(F32) == rank
+    return jnp.concatenate([jnp.where(in_slot, row, 0.0).astype(BF16) for row in rows], axis=0)
+
+
+def prep_kernel(owner_ref, index_ref, rank_ref):
     width = 256
     above = jnp.where(
         sub_iota(width, width) < lax.broadcasted_iota(jnp.int32, (width, width), 1), 1.0, 0.0
@@ -58,46 +61,25 @@
         rank_ref[:, at : at + width] = jnp.sum(hot * before, axis=0, keepdims=True)
         carry = before[:, width - 1 : width] + hot[:, width - 1 : width]
     owner_hot = hot_of(owner_ref[...], DEV).astype(BF16)
-    in_slot = sub_iota(CAP, TILES).astype(F32) == rank_ref[...]
     tile = lax.broadcasted_iota(jnp.int32, (1, TILES), 1)
-
-    def placings(*rows):
-        return jnp.concatenate([jnp.where(in_slot, row, 0.0).astype(BF16) for row in rows], axis=0)
-
-    index = mul(placings((tile // 256).astype(F32), (tile % 256).astype(F32)), owner_hot, NT)
+    index = mul(
+        placings(rank_ref[...], (tile // 256).astype(F32), (tile % 256).astype(F32)), owner_hot, NT
+    )
     index_ref[...] = (index[:CAP] * 256.0 + index[CAP:]).astype(jnp.int32)
-    obs_hot = hot_of(obs_ref[...], OBS).astype(BF16)
-    dir_tile = mul(jnp.broadcast_to(dir_ref[...], (8, OBS)).astype(BF16), obs_hot)[0:1, :]
-    fields = mul(
-        owner_hot,
-        placings(dir_tile, block_ref[...].astype(F32), step_ref[...].astype(F32)),
-        NT,
-    ).astype(BF16)
-    lane_base = lax.axis_index("tm") % 4 * CAP
-    shift = jnp.where(
-        sub_iota(CAP, LANES) + lane_base == lax.broadcasted_iota(jnp.int32, (CAP, LANES), 1),
-        1.0,
-        0.0,
-    ).astype(BF16)
-    meta_ref[:, 0, :] = mul(fields[:, :CAP], shift)
-    meta_ref[:, 1, :] = (
-        mul(fields[:, CAP : 2 * CAP], shift) * 128.0 + mul(fields[:, 2 * CAP :], shift)
-    )
-
-
-def prep(*operands):
+
+
+def prep(owner):
     vmem = pl.BlockSpec(memory_space=pltpu.VMEM)
     return pl.pallas_call(
         prep_kernel,
         out_shape=(
             jax.ShapeDtypeStruct((CAP, DEV), jnp.int32),
-            jax.ShapeDtypeStruct((DEV, 2, LANES), F32),
             jax.ShapeDtypeStruct((1, TILES), F32),
         ),
-        in_specs=[vmem] * 5,
-        out_specs=(vmem,) * 3,
+        in_specs=[vmem],
+        out_specs=(vmem, vmem),
         name="prep",
-    )(*operands)
+    )(owner)
 
 
 def main_kernel(
@@ -105,16 +87,20 @@
     dir_ref,
     noise_ref,
     owner_ref,
+    block_ref,
+    step_ref,
     obs_ref,
     rank_ref,
     index_ref,
+    foot_hbm,
+    cov_hbm,
+    time_hbm,
+    applied_ref,
+    size_ref,
+    ratio_ref,
+    foot_ref,
+    time_ref,
     meta_ref,
-    foot_ref,
-    cov_hbm,
-    time_ref,
-    applied_ref,
-    step_ref,
-    ratio_ref,
     wide,
     slots,
     values,
@@ -138,6 +124,9 @@
     by_rank,
     sums,
     sums_in,
+    ready,
+    foot_sem,
+    time_sem,
     cov_sem,
     tile_send,
     tile_recv,
@@ -205,17 +194,47 @@
         lax.fori_loop(0, 8, at_cell, 0)
 
     barrier = pltpu.get_barrier_semaphore()
-    to_others(
-        lambda to_cell, to_tm: pl.semaphore_signal(
-            barrier, inc=1, device_id=(to_cell, to_tm), device_id_type=MESH
-        )
-    )
+    columns = [(cell + k) % 8 for k in (4, 5, 3, 6, 2, 7, 1)]
+
+    def signal(sem, to_cell, to_tm):
+        pl.semaphore_signal(sem, inc=1, device_id=(to_cell, to_tm), device_id_type=MESH)
+
+    for to_tm in planes[:15]:
+        signal(barrier, cell, to_tm)
+    for to_cell in columns:
+        signal(barrier, to_cell, tm)
+    foot_copy = pltpu.make_async_copy(foot_hbm, foot_ref, foot_sem)
+    foot_copy.start()
+    time_copy = pltpu.make_async_copy(time_hbm, time_ref, time_sem)
+    time_copy.start()
     for k in range(8):
         rows = pl.ds(k * 144, 144)
         pltpu.make_async_copy(cov_hbm.at[rows], cov.at[rows], cov_sem).start()
-
+    pl.semaphore_wait(barrier, 22)
+    for to_cell in columns:
+        signal(ready, to_cell, tm)
+
+    owner_hot = hot_of(owner_ref[...], DEV).astype(BF16)
+    obs_hot = hot_of(obs_ref[...], OBS).astype(BF16)
+    dir_tile = mul(jnp.broadcast_to(dir_ref[...], (8, OBS)).astype(BF16), obs_hot)[0:1, :]
+    fields = mul(
+        owner_hot,
+        placings(rank_ref[...], dir_tile, block_ref[...].astype(F32), step_ref[...].astype(F32)),
+        NT,
+    ).astype(BF16)
+    lane_base = x * CAP
+    shift = jnp.where(
+        sub_iota(CAP, LANES) + lane_base == lax.broadcasted_iota(jnp.int32, (CAP, LANES), 1),
+        1.0,
+        0.0,
+    ).astype(BF16)
+    meta_ref[:, 0, :] = mul(fields[:, :CAP], shift)
+    meta_ref[:, 1, :] = (
+        mul(fields[:, CAP : 2 * CAP], shift) * 128.0 + mul(fields[:, 2 * CAP :], shift)
+    )
+    foot_copy.wait()
     wide[...] = foot_ref[...].astype(F32)
-    pl.semaphore_wait(barrier, DEV - 1)
+    pl.semaphore_wait(ready, 7)
 
     def send_tile(to_cell, to_tm):
         peer = to_cell * 16 + to_tm
@@ -296,6 +315,7 @@
     z_go(cell, left, down, 3)
     z_go(cell, full, partner, 4)
 
+    time_copy.wait()
     time_sends = []
     for k in (1, 2, 3):
         peer = y_at(k)
@@ -496,7 +516,6 @@
     in_slot = sub_iota(CAP, TILES).astype(F32) == rank_ref[...]
     arrived(dots_back.at[pl.ds(0, DEV - 1)], back_recv)
     by_rank[...] = dots_back[:, 0, :].T
-    lane_base = x * CAP
     own = jnp.concatenate(split3(by_rank[pl.ds(pl.multiple_of(lane_base, CAP), CAP), :]), axis=0)
     parts = mul(own, owner_hot)
     tile_dots = jnp.sum(
@@ -535,7 +554,7 @@
     step_size = norm_now / curvature
     norm_next = norm_now - 2.0 * step_size * cross_term + step_size * step_size * image_norm
     applied_ref[...] = applied
-    step_ref[...] = jnp.broadcast_to(step_size, (1, OBS))
+    size_ref[...] = jnp.broadcast_to(step_size, (1, OBS))
     ratio_ref[...] = jnp.broadcast_to(norm_next / norm_now, (1, OBS))
 
     arrived(values.at[pl.ds(0, DEV - 1)], tile_send)
@@ -553,11 +572,14 @@
     return pl.pallas_call(
         main_kernel,
         out_shape=(row, row, row),
-        in_specs=[vmem] * 6
-        + [pl.BlockSpec(memory_space=pltpu.SMEM), vmem, vmem]
-        + [pl.BlockSpec(memory_space=pl.ANY), vmem],
+        in_specs=[vmem] * 8
+        + [pl.BlockSpec(memory_space=pltpu.SMEM)]
+        + [pl.BlockSpec(memory_space=pl.ANY)] * 3,
         out_specs=(vmem,) * 3,
         scratch_shapes=[
+            pltpu.VMEM((TILES, LANES), BF16),
+            pltpu.VMEM((LANES, 16 * LANES), BF16),
+            pltpu.VMEM((DEV, 2, LANES), F32),
             pltpu.VMEM((TILES, LANES), F32),
             pltpu.VMEM((16, CAP, LANES), F32),
             pltpu.VMEM((DEV, CAP, LANES), BF16),
@@ -581,6 +603,9 @@
             pltpu.VMEM((LANES, DEV), F32),
             pltpu.VMEM((1, LANES), F32),
             pltpu.VMEM((DEV, 1, LANES), F32),
+            pltpu.SemaphoreType.REGULAR,
+            dma,
+            dma,
             dma,
             dma,
             dma((8,)),
@@ -621,17 +646,18 @@
 ):
     row = functools.partial(jnp.reshape, shape=(1, OBS))
     tile_row = functools.partial(jnp.reshape, shape=(1, TILES))
-    owner, obs = tile_row(tile_owner), tile_row(tile_obs)
-    index, meta, rank = prep(owner, tile_row(tile_block), tile_row(tile_step), obs, row(direction))
+    owner = tile_row(tile_owner)
+    index, rank = prep(owner)
     outs = whole(
         row(residual),
         row(direction),
         row(noise_var),
         owner,
-        obs,
+        tile_row(tile_block),
+        tile_row(tile_step),
+        tile_row(tile_obs),
         rank,
         index,
-        meta,
         footprints,
         cell_cov,
         time_cov,

time: 88.6 us -> 89.4 us (level)
    pallas_call x1, Pallas kernels: 83.5 us -> 85 us  [whole(): pl.pallas_call(main_kernel, out_shape=(row, row, row), in_specs=[vmem] *...]
where the time goes in v4:
time: 89.4 us; the launch traced here: 89.2 us
  Pallas kernels  87.2 us (98%)
  other arithmetic  1.25 us (1%)
    pallas_call x1, Pallas kernels, whole(): pl.pallas_call(main_kernel, out_shape=(row, row, row), in_specs=[vmem] *...  85 us
    pallas_call x1, Pallas kernels, prep(): pl.pallas_call(prep_kernel, out_shape=(jax.ShapeDtypeStruct((CAP, DEV), j...  2.26 us

profile of v4, /device:TPU:1, one launch (start us, length us, event | category | flops | bytes accessed | tf_op | source)
XLA Modules:
  0.0 89.2 jit_solution(9497504443253711680)
XLA Ops:
  0.6 0.0 copy-start.1
  0.6 0.0 copy-start
  0.7 0.0 copy-start.2
  0.7 2.3 %prep.1 = (s32[32,128]{1,0:T(8,128)}, f32[1,2048]{1,0:T(1,128)}) custom-call(s32[1,2048]{1,0:T(1,128)} %bitcast.10), custom_call_target="tpu_custom_call" | custom-call | tf_op jit(solution)/shard_map/prep/pallas_call | solution.py:73
  2.9 85.0 %whole.1 = (f32[1,256]{1,0:T(1,128)}, f32[1,256]{1,0:T(1,128)}, f32[1,256]{1,0:T(1,128)}) custom-call(f32[1,256]{1,0:T(1,128)} %bitcast.15, f32[1,256]{1,0:T(1,128)} %bitcast.16, f32[1,256]{1,0:T(1,128)} %bitcast.17, s32[1,2048]{1,0:T(1,128)} %bitcast.11, s32[1,2048]{1,0:T(1,128)} %bitcast.12, s32[1,2048]{1,0:T(1,128)} %bitcast.13, s32[1,2048]{1,0:T(1,128)} %bitcast.14, ...), custom_call_target="tpu_custom_call" | custom-call | tf_op jit(solution)/shard_map/whole/pallas_call | solution.py:572
  87.9 0.0 copy-done.1
  87.9 0.0 copy-done
  87.9 0.0 copy-done.2
  87.9 1.2 %multiply_add_fusion = (f32[256]{0:T(256)}, f32[256]{0:T(256)}, f32[256]{0:T(256)}) fusion(f32[256]{0:T(256)} %bitcast.20, f32[256]{0:T(256)S(1)} %copy-done.1, f32[256]{0:T(256)S(1)} %copy-done, f32[256]{0:T(256)} %bitcast.19, f32[256]{0:T(256)} %bitcast.18, f32[256]{0:T(256)S(1)} %copy-done.2), kind=kLoop, calls=%fused_computation | loop fusion | flops 1536 | bytes 9216 | tf_op jit(solution)/shard_map/add | solution.py:667
Async XLA Ops:
  0.6 87.3 %copy-start.1 = (f32[256]{0:T(256)S(1)}, f32[256]{0:T(256)}, u32[]{:S(2)}) copy-start(f32[256]{0:T(256)} %param.13) | copy-start | bytes 3076
  0.6 87.3 %copy-start = (f32[256]{0:T(256)S(1)}, f32[256]{0:T(256)}, u32[]{:S(2)}) copy-start(f32[256]{0:T(256)} %param.12) | copy-start | bytes 3076
  0.7 87.3 %copy-start.2 = (f32[256]{0:T(256)S(1)}, f32[256]{0:T(256)}, u32[]{:S(2)}) copy-start(f32[256]{0:T(256)} %param.11) | copy-start | bytes 3076

commit v5 on v4

--- a/solution.py
+++ b/solution.py
@@ -107,6 +107,7 @@
     cov,
     got,
     got_meta,
+    hots,
     acc,
     flux,
     mixed,
@@ -119,6 +120,7 @@
     in_a,
     in_b,
     smooth,
+    products,
     dots,
     dots_back,
     by_rank,
@@ -179,19 +181,19 @@
     def arrived(ref, sem):
         pltpu.make_async_copy(ref, ref, sem).wait()
 
+    def away(k):
+        return (cell + 4 + (k % 2 * 2 - 1) * ((k + 1) // 2)) % 8
+
     def to_others(send):
         def at_cell(k, _):
-            to_cell = (cell + 4 + k) % 8
-            for to_tm in planes[:15]:
+            to_cell = away(k)
+            for to_tm in planes:
                 send(to_cell, to_tm)
-
-            @pl.when(k != 4)
-            def _():
-                send(to_cell, planes[15])
-
             return 0
 
-        lax.fori_loop(0, 8, at_cell, 0)
+        lax.fori_loop(0, 7, at_cell, 0)
+        for to_tm in planes[:15]:
+            send(cell, to_tm)
 
     barrier = pltpu.get_barrier_semaphore()
     columns = [(cell + k) % 8 for k in (4, 5, 3, 6, 2, 7, 1)]
@@ -245,23 +247,34 @@
             meta_ref.at[peer], got_meta.at[me], meta_send, meta_recv.at[cell], to_cell, to_tm
         ).start()
 
+    def turn(k):
+        q = k % 4
+        return 2 * (q + q // 2 - 2 * (q // 3)) + k // 4
+
+    natural = [ys[dy] * 4 + xs[dx] for dy in range(4) for dx in range(4)]
+
+    def gather(to_cell, j):
+        peer = to_cell * 16 + natural[j]
+        for r in range(CAP):
+            slots[j, r : r + 1, :] = wide[pl.ds(index_ref[r, peer], 1), :]
+        values[peer] = slots[j].astype(BF16)
+
+    for j in range(16):
+        gather(cell, j)
+        if j > 1:
+            send_tile(cell, natural[j - 1])
+    send_tile(cell, natural[15])
+
     def gather_and_send(k, _):
-        to_cell = (cell + 4 + k) % 8
+        to_cell = (cell + turn(k)) % 8
         for j in range(16):
-            peer = to_cell * 16 + planes[j]
-            for r in range(CAP):
-                slots[j, r : r + 1, :] = wide[pl.ds(index_ref[r, peer], 1), :]
-            values[peer] = slots[j].astype(BF16)
+            gather(to_cell, j)
             if j:
-                send_tile(to_cell, planes[j - 1])
-
-        @pl.when(k != 4)
-        def _():
-            send_tile(to_cell, planes[15])
-
+                send_tile(to_cell, natural[j - 1])
+        send_tile(to_cell, natural[15])
         return 0
 
-    lax.fori_loop(0, 8, gather_and_send, 0)
+    lax.fori_loop(1, 8, gather_and_send, 0)
     pltpu.make_async_copy(values.at[me], got.at[me], tile_recv.at[cell]).start()
     pltpu.make_async_copy(meta_ref.at[me], got_meta.at[me], meta_recv.at[cell]).start()
 
@@ -273,22 +286,17 @@
         return jnp.sum(rows.reshape(4, 4, 2, LANES), axis=1)
 
     def add_group(k, _):
-        group = (cell + 12 - k) % 8
+        group = (cell + 8 - turn(k)) % 8
         arrived(got.at[pl.ds(group * 16, 16)], tile_recv.at[group])
         arrived(got_meta.at[pl.ds(group * 16, 16)], meta_recv.at[group])
         rows = load_meta(group)
         tiles = got[pl.ds(group * 16, 16)].reshape(512, LANES)
         for b in range(BLOCKS):
-            hot = jnp.concatenate(
-                [
-                    jnp.where(row_of + b * 128.0 == rows[q, 1:2, :], rows[q, 0:1, :], 0.0).astype(
-                        BF16
-                    )
-                    for q in range(4)
-                ],
-                axis=1,
-            )
-            acc[b * 128 : b * 128 + 128, :] += mul(hot, tiles)
+            for q in range(4):
+                hots[b * 128 : b * 128 + 128, q * 128 : q * 128 + 128] = jnp.where(
+                    row_of + b * 128.0 == rows[q, 1:2, :], rows[q, 0:1, :], 0.0
+                ).astype(BF16)
+        acc[...] += mul(hots[...], tiles)
         return 0
 
     lax.fori_loop(0, 8, add_group, 0)
@@ -472,44 +480,38 @@
         arrived(in_b.at[k - 1], rs_recv.at[k + 2])
         mixed[HALF:, :] += in_b[k - 1].astype(F32)
     for b in range(BLOCKS):
-        smooth[b] = mixed[b * 128 : b * 128 + 128, :].T.astype(BF16)
-
-    def dot_group(k, _):
-        group = (cell + 4 + k) % 8
+        smooth[b * 128 : b * 128 + 128, :] = mixed[b * 128 : b * 128 + 128, :].T.astype(BF16)
+
+    def dot_group(k):
+        group = away(k)
         rows = load_meta(group)
-        tiles = got[pl.ds(group * 16, 16)].reshape(512, LANES)
-        picked = [jnp.zeros((LANES, LANES), F32) for _ in range(4)]
-        for b in range(BLOCKS):
-            product = mul(smooth[b], tiles, NT)
-            for q in range(4):
-                picked[q] += jnp.where(
+        products[...] = mul(smooth[...], got[pl.ds(group * 16, 16)].reshape(512, LANES), NT)
+        for q in range(4):
+            picked = jnp.zeros((LANES, LANES), F32)
+            for b in range(BLOCKS):
+                picked += jnp.where(
                     row_of + b * 128.0 == rows[q, 1:2, :],
-                    product[:, q * 128 : q * 128 + 128],
+                    products[b * 128 : b * 128 + 128, q * 128 : q * 128 + 128],
                     0.0,
                 )
-        for q in range(4):
-            dots[group * 4 + q] = jnp.sum(picked[q], axis=0, keepdims=True)
-
-        def send_dots(to_tm):
+            dots[group * 4 + q] = jnp.sum(picked, axis=0, keepdims=True)
+
+    def send_dots(k, peers):
+        group = away(k)
+        for to_tm in peers:
             remote(
-                dots.at[group * 4 + to_tm // 4],
-                dots_back.at[me],
-                back_send,
-                back_recv,
-                group,
-                to_tm,
+                dots.at[group * 4 + to_tm // 4], dots_back.at[me], back_send, back_recv, group, to_tm
             ).start()
 
-        for to_tm in planes[:15]:
-            send_dots(to_tm)
-
-        @pl.when(k != 4)
-        def _():
-            send_dots(planes[15])
-
+    dot_group(0)
+
+    def dots_and_send(k, _):
+        send_dots(k - 1, planes)
+        dot_group(k)
         return 0
 
-    lax.fori_loop(0, 8, dot_group, 0)
+    lax.fori_loop(1, 8, dots_and_send, 0)
+    send_dots(7, planes[:15])
     dots_back[me] = dots[me // 4]
     owner_hot = hot_of(owner_ref[...], DEV).astype(BF16)
     obs_hot = hot_of(obs_ref[...], OBS).astype(BF16)
@@ -586,6 +588,7 @@
             pltpu.VMEM((ROWS, 8 * ROWS), BF16),
             pltpu.VMEM((DEV, CAP, LANES), BF16),
             pltpu.VMEM((DEV, 2, LANES), F32),
+            pltpu.VMEM((ROWS, 512), BF16),
             pltpu.VMEM((ROWS, LANES), F32),
             pltpu.VMEM((8, LANES, ROWS), BF16),
             pltpu.VMEM((ROWS, LANES), F32),
@@ -597,7 +600,8 @@
             pltpu.VMEM((3, HALF, LANES), BF16),
             pltpu.VMEM((3, HALF, LANES), BF16),
             pltpu.VMEM((3, HALF, LANES), BF16),
-            pltpu.VMEM((BLOCKS, LANES, LANES), BF16),
+            pltpu.VMEM((ROWS, LANES), BF16),
+            pltpu.VMEM((ROWS, 512), F32),
             pltpu.VMEM((DEV // 4, 1, LANES), F32),
             pltpu.VMEM((DEV, 1, LANES), F32),
             pltpu.VMEM((LANES, DEV), F32),

time: 89.4 us -> 88.3 us (0.988)
  Pallas kernels: 87.2 us -> 86.1 us
    pallas_call x1, Pallas kernels: 85 us -> 83.8 us  [whole(): pl.pallas_call(main_kernel, out_shape=(row, row, row), in_specs=[vmem] *...]
where the time goes in v5:
time: 88.3 us; the launch traced here: 88.1 us
  Pallas kernels  86.1 us (98%)
  other arithmetic  1.25 us (1%)
    pallas_call x1, Pallas kernels, whole(): pl.pallas_call(main_kernel, out_shape=(row, row, row), in_specs=[vmem] *...  83.8 us
    pallas_call x1, Pallas kernels, prep(): pl.pallas_call(prep_kernel, out_shape=(jax.ShapeDtypeStruct((CAP, DEV), j...  2.27 us

profile of v5, /device:TPU:1, one launch (start us, length us, event | category | flops | bytes accessed | tf_op | source)
XLA Modules:
  0.0 88.1 jit_solution(15250005785913468962)
XLA Ops:
  0.6 0.0 copy-start.1
  0.6 0.0 copy-start
  0.7 0.0 copy-start.2
  0.7 2.3 %prep.1 = (s32[32,128]{1,0:T(8,128)}, f32[1,2048]{1,0:T(1,128)}) custom-call(s32[1,2048]{1,0:T(1,128)} %bitcast.10), custom_call_target="tpu_custom_call" | custom-call | tf_op jit(solution)/shard_map/prep/pallas_call | solution.py:73
  2.9 83.8 %whole.1 = (f32[1,256]{1,0:T(1,128)}, f32[1,256]{1,0:T(1,128)}, f32[1,256]{1,0:T(1,128)}) custom-call(f32[1,256]{1,0:T(1,128)} %bitcast.15, f32[1,256]{1,0:T(1,128)} %bitcast.16, f32[1,256]{1,0:T(1,128)} %bitcast.17, s32[1,2048]{1,0:T(1,128)} %bitcast.11, s32[1,2048]{1,0:T(1,128)} %bitcast.12, s32[1,2048]{1,0:T(1,128)} %bitcast.13, s32[1,2048]{1,0:T(1,128)} %bitcast.14, ...), custom_call_target="tpu_custom_call" | custom-call | tf_op jit(solution)/shard_map/whole/pallas_call | solution.py:574
  86.8 0.0 copy-done.1
  86.8 0.0 copy-done
  86.8 0.0 copy-done.2
  86.8 1.2 %multiply_add_fusion = (f32[256]{0:T(256)}, f32[256]{0:T(256)}, f32[256]{0:T(256)}) fusion(f32[256]{0:T(256)} %bitcast.20, f32[256]{0:T(256)S(1)} %copy-done.1, f32[256]{0:T(256)S(1)} %copy-done, f32[256]{0:T(256)} %bitcast.19, f32[256]{0:T(256)} %bitcast.18, f32[256]{0:T(256)S(1)} %copy-done.2), kind=kLoop, calls=%fused_computation | loop fusion | flops 1536 | bytes 9216 | tf_op jit(solution)/shard_map/add | solution.py:671
Async XLA Ops:
  0.6 86.2 %copy-start.1 = (f32[256]{0:T(256)S(1)}, f32[256]{0:T(256)}, u32[]{:S(2)}) copy-start(f32[256]{0:T(256)} %param.13) | copy-start | bytes 3076
  0.6 86.2 %copy-start = (f32[256]{0:T(256)S(1)}, f32[256]{0:T(256)}, u32[]{:S(2)}) copy-start(f32[256]{0:T(256)} %param.12) | copy-start | bytes 3076
  0.7 86.2 %copy-start.2 = (f32[256]{0:T(256)S(1)}, f32[256]{0:T(256)}, u32[]{:S(2)}) copy-start(f32[256]{0:T(256)} %param.11) | copy-start | bytes 3076

commit v6 on v5

--- a/solution.py
+++ b/solution.py
@@ -225,14 +225,16 @@
         NT,
     ).astype(BF16)
     lane_base = x * CAP
-    shift = jnp.where(
-        sub_iota(CAP, LANES) + lane_base == lax.broadcasted_iota(jnp.int32, (CAP, LANES), 1),
-        1.0,
-        0.0,
-    ).astype(BF16)
-    meta_ref[:, 0, :] = mul(fields[:, :CAP], shift)
-    meta_ref[:, 1, :] = (
-        mul(fields[:, CAP : 2 * CAP], shift) * 128.0 + mul(fields[:, 2 * CAP :], shift)
+    lane = lax.broadcasted_iota(jnp.int32, (CAP, LANES), 1)
+
+    def to_quarter(value, quarter):
+        hot = jnp.where(sub_iota(CAP, LANES) + quarter * CAP == lane, 1.0, 0.0)
+        return mul(value, hot.astype(BF16))
+
+    meta_ref[:, 0, :] = (
+        to_quarter(fields[:, :CAP], x)
+        + to_quarter(fields[:, CAP : 2 * CAP], xs[2]) * 128.0
+        + to_quarter(fields[:, 2 * CAP :], xs[2])
     )
     foot_copy.wait()
     wide[...] = foot_ref[...].astype(F32)
@@ -281,9 +283,21 @@
     acc[...] = jnp.zeros_like(acc)
     row_of = sub_iota(LANES, LANES).astype(F32)
 
+    quarter_of = lax.broadcasted_iota(jnp.int32, (1, LANES), 1) // CAP
+
     def load_meta(group):
-        rows = got_meta[pl.ds(group * 16, 16)]
-        return jnp.sum(rows.reshape(4, 4, 2, LANES), axis=1)
+        rows = got_meta[pl.ds(group * 16, 16)].reshape(4, 4, LANES)
+        out = []
+        for q in range(4):
+            direction = place = jnp.zeros((1, LANES), F32)
+            for j in range(4):
+                row = rows[q, j : j + 1, :]
+                direction = jnp.where(quarter_of == j, row, direction)
+                place = jnp.where(quarter_of == (j + 2) % 4, row, place)
+            place = jnp.concatenate([place[:, 64:], place[:, :64]], axis=1)
+            block = jnp.floor(place * (1.0 / 128.0))
+            out.append((direction, block, place - block * 128.0))
+        return out
 
     def add_group(k, _):
         group = (cell + 8 - turn(k)) % 8
@@ -291,10 +305,11 @@
         arrived(got_meta.at[pl.ds(group * 16, 16)], meta_recv.at[group])
         rows = load_meta(group)
         tiles = got[pl.ds(group * 16, 16)].reshape(512, LANES)
-        for b in range(BLOCKS):
-            for q in range(4):
-                hots[b * 128 : b * 128 + 128, q * 128 : q * 128 + 128] = jnp.where(
-                    row_of + b * 128.0 == rows[q, 1:2, :], rows[q, 0:1, :], 0.0
+        for q, (direction, block, step) in enumerate(rows):
+            hot = jnp.where(row_of == step, direction, 0.0).astype(BF16)
+            for b in range(BLOCKS):
+                hots[b * 128 : b * 128 + 128, q * 128 : q * 128 + 128] = hot * jnp.where(
+                    block == b, 1.0, 0.0
                 ).astype(BF16)
         acc[...] += mul(hots[...], tiles)
         return 0
@@ -486,14 +501,12 @@
         group = away(k)
         rows = load_meta(group)
         products[...] = mul(smooth[...], got[pl.ds(group * 16, 16)].reshape(512, LANES), NT)
-        for q in range(4):
-            picked = jnp.zeros((LANES, LANES), F32)
-            for b in range(BLOCKS):
-                picked += jnp.where(
-                    row_of + b * 128.0 == rows[q, 1:2, :],
-                    products[b * 128 : b * 128 + 128, q * 128 : q * 128 + 128],
-                    0.0,
-                )
+        for q, (_, block, step) in enumerate(rows):
+            cols = slice(q * 128, q * 128 + 128)
+            picked = products[0:128, cols]
+            for b in range(1, BLOCKS):
+                picked = jnp.where(block == b, products[b * 128 : b * 128 + 128, cols], picked)
+            picked = jnp.where(row_of == step, picked, 0.0)
             dots[group * 4 + q] = jnp.sum(picked, axis=0, keepdims=True)
 
     def send_dots(k, peers):
@@ -581,13 +594,13 @@
         scratch_shapes=[
             pltpu.VMEM((TILES, LANES), BF16),
             pltpu.VMEM((LANES, 16 * LANES), BF16),
-            pltpu.VMEM((DEV, 2, LANES), F32),
+            pltpu.VMEM((DEV, 1, LANES), F32),
             pltpu.VMEM((TILES, LANES), F32),
             pltpu.VMEM((16, CAP, LANES), F32),
             pltpu.VMEM((DEV, CAP, LANES), BF16),
             pltpu.VMEM((ROWS, 8 * ROWS), BF16),
             pltpu.VMEM((DEV, CAP, LANES), BF16),
-            pltpu.VMEM((DEV, 2, LANES), F32),
+            pltpu.VMEM((DEV, 1, LANES), F32),
             pltpu.VMEM((ROWS, 512), BF16),
             pltpu.VMEM((ROWS, LANES), F32),
             pltpu.VMEM((8, LANES, ROWS), BF16),

time: 88.3 us -> 87.4 us (0.990)
  Pallas kernels: 86.1 us -> 85.2 us
    pallas_call x1, Pallas kernels: 83.8 us -> 82.9 us  [whole(): pl.pallas_call(main_kernel, out_shape=(row, row, row), in_specs=[vmem] *...]
where the time goes in v6:
time: 87.4 us; the launch traced here: 87.1 us
  Pallas kernels  85.2 us (97%)
  other arithmetic  1.25 us (1%)
    pallas_call x1, Pallas kernels, whole(): pl.pallas_call(main_kernel, out_shape=(row, row, row), in_specs=[vmem] *...  82.9 us
    pallas_call x1, Pallas kernels, prep(): pl.pallas_call(prep_kernel, out_shape=(jax.ShapeDtypeStruct((CAP, DEV), j...  2.27 us

profile of v6, /device:TPU:1, one launch (start us, length us, event | category | flops | bytes accessed | tf_op | source)
XLA Modules:
  0.0 87.1 jit_solution(18260830816812729134)
XLA Ops:
  0.6 0.0 copy-start.1
  0.6 0.0 copy-start
  0.7 0.0 copy-start.2
  0.7 2.3 %prep.1 = (s32[32,128]{1,0:T(8,128)}, f32[1,2048]{1,0:T(1,128)}) custom-call(s32[1,2048]{1,0:T(1,128)} %bitcast.10), custom_call_target="tpu_custom_call" | custom-call | tf_op jit(solution)/shard_map/prep/pallas_call | solution.py:73
  2.9 82.9 %whole.1 = (f32[1,256]{1,0:T(1,128)}, f32[1,256]{1,0:T(1,128)}, f32[1,256]{1,0:T(1,128)}) custom-call(f32[1,256]{1,0:T(1,128)} %bitcast.15, f32[1,256]{1,0:T(1,128)} %bitcast.16, f32[1,256]{1,0:T(1,128)} %bitcast.17, s32[1,2048]{1,0:T(1,128)} %bitcast.11, s32[1,2048]{1,0:T(1,128)} %bitcast.12, s32[1,2048]{1,0:T(1,128)} %bitcast.13, s32[1,2048]{1,0:T(1,128)} %bitcast.14, ...), custom_call_target="tpu_custom_call" | custom-call | tf_op jit(solution)/shard_map/whole/pallas_call | solution.py:587
  85.9 0.0 copy-done.1
  85.9 0.0 copy-done
  85.9 0.0 copy-done.2
  85.9 1.2 %multiply_add_fusion = (f32[256]{0:T(256)}, f32[256]{0:T(256)}, f32[256]{0:T(256)}) fusion(f32[256]{0:T(256)} %bitcast.20, f32[256]{0:T(256)S(1)} %copy-done.1, f32[256]{0:T(256)S(1)} %copy-done, f32[256]{0:T(256)} %bitcast.19, f32[256]{0:T(256)} %bitcast.18, f32[256]{0:T(256)S(1)} %copy-done.2), kind=kLoop, calls=%fused_computation | loop fusion | flops 1536 | bytes 9216 | tf_op jit(solution)/shard_map/add | solution.py:684
Async XLA Ops:
  0.6 85.2 %copy-start.1 = (f32[256]{0:T(256)S(1)}, f32[256]{0:T(256)}, u32[]{:S(2)}) copy-start(f32[256]{0:T(256)} %param.13) | copy-start | bytes 3076
  0.6 85.2 %copy-start = (f32[256]{0:T(256)S(1)}, f32[256]{0:T(256)}, u32[]{:S(2)}) copy-start(f32[256]{0:T(256)} %param.12) | copy-start | bytes 3076
  0.7 85.2 %copy-start.2 = (f32[256]{0:T(256)S(1)}, f32[256]{0:T(256)}, u32[]{:S(2)}) copy-start(f32[256]{0:T(256)} %param.11) | copy-start | bytes 3076

commit v7 on v6

--- a/solution.py
+++ b/solution.py
@@ -107,6 +107,7 @@
     cov,
     got,
     got_meta,
+    places,
     hots,
     acc,
     flux,
@@ -306,6 +307,8 @@
         rows = load_meta(group)
         tiles = got[pl.ds(group * 16, 16)].reshape(512, LANES)
         for q, (direction, block, step) in enumerate(rows):
+            places[group * 4 + q, 0:1, :] = block
+            places[group * 4 + q, 1:2, :] = step
             hot = jnp.where(row_of == step, direction, 0.0).astype(BF16)
             for b in range(BLOCKS):
                 hots[b * 128 : b * 128 + 128, q * 128 : q * 128 + 128] = hot * jnp.where(
@@ -320,7 +323,8 @@
 
     partner = z * 2 + 1 - core
     up, down, far = z_cell(1), z_cell(3), z_cell(2)
-    left, right, full = pl.ds(0, 512), pl.ds(512, ROWS - 512), pl.ds(0, ROWS)
+    full = pl.ds(0, ROWS)
+    pieces = [pl.ds(0, 256), pl.ds(256, 256), pl.ds(512, 384), pl.ds(896, 256)]
     z_copies = []
 
     def z_go(block, cols, to_cell, at):
@@ -332,11 +336,10 @@
     def z_wait(block, cols, at):
         arrived(flux.at[block, :, cols], z_recv.at[at])
 
-    z_go(cell, left, up, 0)
-    z_go(cell, right, down, 2)
-    z_go(cell, right, up, 1)
-    z_go(cell, left, down, 3)
-    z_go(cell, full, partner, 4)
+    for i in range(4):
+        z_go(cell, pieces[i], up, i)
+        z_go(cell, pieces[3 - i], down, 7 - i)
+    z_go(cell, full, partner, 12)
 
     time_copy.wait()
     time_sends = []
@@ -375,43 +378,42 @@
     def other_core(c):
         return c // 2 * 2 + 1 - c % 2
 
-    def mix(block, first=False):
-        cols = pl.ds(pl.multiple_of(block * ROWS, 128), ROWS)
-        product = mul(cov[:, cols], flux[block], NT)
+    def mix(block, piece=full, first=False):
+        cols = pl.ds(pl.multiple_of(block * ROWS + piece.start, 128), piece.size)
+        product = mul(cov[:, cols], flux[block, :, piece], NT)
         if first:
             mixed[...] = product
         else:
             mixed[...] += product
 
-    mix(cell, True)
-    z_wait(down, left, 0)
-    z_go(down, left, up, 5)
-    z_go(down, left, partner, 7)
-    z_wait(up, right, 2)
-    z_go(up, right, down, 6)
-    z_go(up, right, partner, 8)
-    z_wait(other_core(cell), full, 4)
+    mix(cell, first=True)
+    for i in (0, 1):
+        z_wait(down, pieces[i], i)
+        z_go(down, pieces[i], up, 8 + i)
+        z_go(down, pieces[i], partner, 13 + i)
+        z_wait(up, pieces[3 - i], 7 - i)
+        z_go(up, pieces[3 - i], down, 11 - i)
+        z_go(up, pieces[3 - i], partner, 20 - i)
+    z_wait(other_core(cell), full, 12)
     mix(other_core(cell))
-    z_wait(down, right, 1)
-    z_go(down, right, partner, 9)
-    z_wait(up, left, 3)
-    z_go(up, left, partner, 10)
+    for i in (2, 3):
+        z_wait(down, pieces[i], i)
+        z_go(down, pieces[i], partner, 13 + i)
+        z_wait(up, pieces[3 - i], 7 - i)
+        z_go(up, pieces[3 - i], partner, 20 - i)
     mix(down)
     mix(up)
-    z_wait(other_core(down), left, 7)
-    z_wait(other_core(down), right, 9)
-    mix(other_core(down))
-    z_wait(other_core(up), right, 8)
-    z_wait(other_core(up), left, 10)
-    mix(other_core(up))
-    z_wait(far, left, 5)
-    z_go(far, left, partner, 11)
-    z_wait(far, right, 6)
-    z_go(far, right, partner, 12)
-    mix(far)
-    z_wait(other_core(far), left, 11)
-    z_wait(other_core(far), right, 12)
-    mix(other_core(far))
+    for block, at in ((other_core(down), 13), (other_core(up), 17)):
+        for i in range(4):
+            z_wait(block, pieces[i], at + i)
+        mix(block)
+    for i in (0, 3, 1, 2):
+        z_wait(far, pieces[i], 8 + i)
+        z_go(far, pieces[i], partner, 21 + i)
+        mix(far, pieces[i])
+    for i in (0, 3, 1, 2):
+        z_wait(other_core(far), pieces[i], 21 + i)
+        mix(other_core(far), pieces[i])
 
     mix_a[:, pl.ds(pl.multiple_of(x * 128, 128), 128)] = mixed[:HALF, :].astype(BF16)
     mix_b[:, pl.ds(pl.multiple_of(y * 128, 128), 128)] = mixed[HALF:, :].astype(BF16)
@@ -499,9 +501,9 @@
 
     def dot_group(k):
         group = away(k)
-        rows = load_meta(group)
         products[...] = mul(smooth[...], got[pl.ds(group * 16, 16)].reshape(512, LANES), NT)
-        for q, (_, block, step) in enumerate(rows):
+        for q in range(4):
+            block, step = places[group * 4 + q, 0:1, :], places[group * 4 + q, 1:2, :]
             cols = slice(q * 128, q * 128 + 128)
             picked = products[0:128, cols]
             for b in range(1, BLOCKS):
@@ -601,6 +603,7 @@
             pltpu.VMEM((ROWS, 8 * ROWS), BF16),
             pltpu.VMEM((DEV, CAP, LANES), BF16),
             pltpu.VMEM((DEV, 1, LANES), F32),
+            pltpu.VMEM((DEV // 4, 2, LANES), F32),
             pltpu.VMEM((ROWS, 512), BF16),
             pltpu.VMEM((ROWS, LANES), F32),
             pltpu.VMEM((8, LANES, ROWS), BF16),
@@ -628,8 +631,8 @@
             dma((8,)),
             dma,
             dma((8,)),
-            dma((13,)),
-            dma((13,)),
+            dma((25,)),
+            dma((25,)),
             dma((15,)),
             dma((15,)),
             dma((12,)),

time: 87.4 us -> 88.5 us (1.013)
  Pallas kernels: 85.2 us -> 86.3 us
    pallas_call x1, Pallas kernels: 82.9 us -> 84 us  [whole(): pl.pallas_call(main_kernel, out_shape=(row, row, row), in_specs=[vmem] *...]
where the time goes in v7:
time: 88.5 us; the launch traced here: 88.2 us
  Pallas kernels  86.3 us (98%)
  other arithmetic  1.25 us (1%)
    pallas_call x1, Pallas kernels, whole(): pl.pallas_call(main_kernel, out_shape=(row, row, row), in_specs=[vmem] *...  84 us
    pallas_call x1, Pallas kernels, prep(): pl.pallas_call(prep_kernel, out_shape=(jax.ShapeDtypeStruct((CAP, DEV), j...  2.27 us

profile of v7, /device:TPU:1, one launch (start us, length us, event | category | flops | bytes accessed | tf_op | source)
XLA Modules:
  0.0 88.2 jit_solution(3494291419451944001)
XLA Ops:
  0.6 0.0 copy-start.1
  0.6 0.0 copy-start
  0.7 0.0 copy-start.2
  0.7 2.3 %prep.1 = (s32[32,128]{1,0:T(8,128)}, f32[1,2048]{1,0:T(1,128)}) custom-call(s32[1,2048]{1,0:T(1,128)} %bitcast.10), custom_call_target="tpu_custom_call" | custom-call | tf_op jit(solution)/shard_map/prep/pallas_call | solution.py:73
  2.9 84.0 %whole.1 = (f32[1,256]{1,0:T(1,128)}, f32[1,256]{1,0:T(1,128)}, f32[1,256]{1,0:T(1,128)}) custom-call(f32[1,256]{1,0:T(1,128)} %bitcast.15, f32[1,256]{1,0:T(1,128)} %bitcast.16, f32[1,256]{1,0:T(1,128)} %bitcast.17, s32[1,2048]{1,0:T(1,128)} %bitcast.11, s32[1,2048]{1,0:T(1,128)} %bitcast.12, s32[1,2048]{1,0:T(1,128)} %bitcast.13, s32[1,2048]{1,0:T(1,128)} %bitcast.14, ...), custom_call_target="tpu_custom_call" | custom-call | tf_op jit(solution)/shard_map/whole/pallas_call | solution.py:589
  87.0 0.0 copy-done.1
  87.0 0.0 copy-done
  87.0 0.0 copy-done.2
  87.0 1.2 %multiply_add_fusion = (f32[256]{0:T(256)}, f32[256]{0:T(256)}, f32[256]{0:T(256)}) fusion(f32[256]{0:T(256)} %bitcast.20, f32[256]{0:T(256)S(1)} %copy-done.1, f32[256]{0:T(256)S(1)} %copy-done, f32[256]{0:T(256)} %bitcast.19, f32[256]{0:T(256)} %bitcast.18, f32[256]{0:T(256)S(1)} %copy-done.2), kind=kLoop, calls=%fused_computation | loop fusion | flops 1536 | bytes 9216 | tf_op jit(solution)/shard_map/add | solution.py:687
Async XLA Ops:
  0.6 86.3 %copy-start.1 = (f32[256]{0:T(256)S(1)}, f32[256]{0:T(256)}, u32[]{:S(2)}) copy-start(f32[256]{0:T(256)} %param.13) | copy-start | bytes 3076
  0.6 86.3 %copy-start = (f32[256]{0:T(256)S(1)}, f32[256]{0:T(256)}, u32[]{:S(2)}) copy-start(f32[256]{0:T(256)} %param.12) | copy-start | bytes 3076
  0.7 86.3 %copy-start.2 = (f32[256]{0:T(256)S(1)}, f32[256]{0:T(256)}, u32[]{:S(2)}) copy-start(f32[256]{0:T(256)} %param.11) | copy-start | bytes 3076

commit v8 on v6

--- a/solution.py
+++ b/solution.py
@@ -107,6 +107,7 @@
     cov,
     got,
     got_meta,
+    places,
     hots,
     acc,
     flux,
@@ -126,7 +127,6 @@
     by_rank,
     sums,
     sums_in,
-    ready,
     foot_sem,
     time_sem,
     cov_sem,
@@ -196,15 +196,11 @@
             send(cell, to_tm)
 
     barrier = pltpu.get_barrier_semaphore()
-    columns = [(cell + k) % 8 for k in (4, 5, 3, 6, 2, 7, 1)]
 
     def signal(sem, to_cell, to_tm):
         pl.semaphore_signal(sem, inc=1, device_id=(to_cell, to_tm), device_id_type=MESH)
 
-    for to_tm in planes[:15]:
-        signal(barrier, cell, to_tm)
-    for to_cell in columns:
-        signal(barrier, to_cell, tm)
+    to_others(lambda to_cell, to_tm: signal(barrier, to_cell, to_tm))
     foot_copy = pltpu.make_async_copy(foot_hbm, foot_ref, foot_sem)
     foot_copy.start()
     time_copy = pltpu.make_async_copy(time_hbm, time_ref, time_sem)
@@ -212,9 +208,6 @@
     for k in range(8):
         rows = pl.ds(k * 144, 144)
         pltpu.make_async_copy(cov_hbm.at[rows], cov.at[rows], cov_sem).start()
-    pl.semaphore_wait(barrier, 22)
-    for to_cell in columns:
-        signal(ready, to_cell, tm)
 
     owner_hot = hot_of(owner_ref[...], DEV).astype(BF16)
     obs_hot = hot_of(obs_ref[...], OBS).astype(BF16)
@@ -238,7 +231,7 @@
     )
     foot_copy.wait()
     wide[...] = foot_ref[...].astype(F32)
-    pl.semaphore_wait(ready, 7)
+    pl.semaphore_wait(barrier, DEV - 1)
 
     def send_tile(to_cell, to_tm):
         peer = to_cell * 16 + to_tm
@@ -306,6 +299,8 @@
         rows = load_meta(group)
         tiles = got[pl.ds(group * 16, 16)].reshape(512, LANES)
         for q, (direction, block, step) in enumerate(rows):
+            places[group * 4 + q, 0:1, :] = block
+            places[group * 4 + q, 1:2, :] = step
             hot = jnp.where(row_of == step, direction, 0.0).astype(BF16)
             for b in range(BLOCKS):
                 hots[b * 128 : b * 128 + 128, q * 128 : q * 128 + 128] = hot * jnp.where(
@@ -499,9 +494,9 @@
 
     def dot_group(k):
         group = away(k)
-        rows = load_meta(group)
         products[...] = mul(smooth[...], got[pl.ds(group * 16, 16)].reshape(512, LANES), NT)
-        for q, (_, block, step) in enumerate(rows):
+        for q in range(4):
+            block, step = places[group * 4 + q, 0:1, :], places[group * 4 + q, 1:2, :]
             cols = slice(q * 128, q * 128 + 128)
             picked = products[0:128, cols]
             for b in range(1, BLOCKS):
@@ -601,6 +596,7 @@
             pltpu.VMEM((ROWS, 8 * ROWS), BF16),
             pltpu.VMEM((DEV, CAP, LANES), BF16),
             pltpu.VMEM((DEV, 1, LANES), F32),
+            pltpu.VMEM((DEV // 4, 2, LANES), F32),
             pltpu.VMEM((ROWS, 512), BF16),
             pltpu.VMEM((ROWS, LANES), F32),
             pltpu.VMEM((8, LANES, ROWS), BF16),
@@ -620,7 +616,6 @@
             pltpu.VMEM((LANES, DEV), F32),
             pltpu.VMEM((1, LANES), F32),
             pltpu.VMEM((DEV, 1, LANES), F32),
-            pltpu.SemaphoreType.REGULAR,
             dma,
             dma,
             dma,

time: 87.4 us -> 86.5 us (0.990)
  Pallas kernels: 85.2 us -> 84.3 us
where the time goes in v8:
time: 86.5 us; the launch traced here: 86.3 us
  Pallas kernels  84.3 us (97%)
  other arithmetic  1.25 us (1%)
    pallas_call x1, Pallas kernels, whole(): pl.pallas_call(main_kernel, out_shape=(row, row, row), in_specs=[vmem] *...  82.1 us
    pallas_call x1, Pallas kernels, prep(): pl.pallas_call(prep_kernel, out_shape=(jax.ShapeDtypeStruct((CAP, DEV), j...  2.26 us

profile of v8, /device:TPU:1, one launch (start us, length us, event | category | flops | bytes accessed | tf_op | source)
XLA Modules:
  0.0 86.3 jit_solution(3484972393891470648)
XLA Ops:
  0.6 0.0 copy-start.1
  0.6 0.0 copy-start
  0.7 0.0 copy-start.2
  0.7 2.3 %prep.1 = (s32[32,128]{1,0:T(8,128)}, f32[1,2048]{1,0:T(1,128)}) custom-call(s32[1,2048]{1,0:T(1,128)} %bitcast.10), custom_call_target="tpu_custom_call" | custom-call | tf_op jit(solution)/shard_map/prep/pallas_call | solution.py:73
  2.9 82.1 %whole.1 = (f32[1,256]{1,0:T(1,128)}, f32[1,256]{1,0:T(1,128)}, f32[1,256]{1,0:T(1,128)}) custom-call(f32[1,256]{1,0:T(1,128)} %bitcast.15, f32[1,256]{1,0:T(1,128)} %bitcast.16, f32[1,256]{1,0:T(1,128)} %bitcast.17, s32[1,2048]{1,0:T(1,128)} %bitcast.11, s32[1,2048]{1,0:T(1,128)} %bitcast.12, s32[1,2048]{1,0:T(1,128)} %bitcast.13, s32[1,2048]{1,0:T(1,128)} %bitcast.14, ...), custom_call_target="tpu_custom_call" | custom-call | tf_op jit(solution)/shard_map/whole/pallas_call | solution.py:582
  85.0 0.0 copy-done.1
  85.0 0.0 copy-done
  85.0 0.0 copy-done.2
  85.0 1.2 %multiply_add_fusion = (f32[256]{0:T(256)}, f32[256]{0:T(256)}, f32[256]{0:T(256)}) fusion(f32[256]{0:T(256)} %bitcast.20, f32[256]{0:T(256)S(1)} %copy-done.1, f32[256]{0:T(256)S(1)} %copy-done, f32[256]{0:T(256)} %bitcast.19, f32[256]{0:T(256)} %bitcast.18, f32[256]{0:T(256)S(1)} %copy-done.2), kind=kLoop, calls=%fused_computation | loop fusion | flops 1536 | bytes 9216 | tf_op jit(solution)/shard_map/add | solution.py:679
Async XLA Ops:
  0.6 84.4 %copy-start.1 = (f32[256]{0:T(256)S(1)}, f32[256]{0:T(256)}, u32[]{:S(2)}) copy-start(f32[256]{0:T(256)} %param.13) | copy-start | bytes 3076
  0.6 84.4 %copy-start = (f32[256]{0:T(256)S(1)}, f32[256]{0:T(256)}, u32[]{:S(2)}) copy-start(f32[256]{0:T(256)} %param.12) | copy-start | bytes 3076
  0.7 84.4 %copy-start.2 = (f32[256]{0:T(256)S(1)}, f32[256]{0:T(256)}, u32[]{:S(2)}) copy-start(f32[256]{0:T(256)} %param.11) | copy-start | bytes 3076

commit v9 on v8

--- a/solution.py
+++ b/solution.py
@@ -185,13 +185,10 @@
         return (cell + 4 + (k % 2 * 2 - 1) * ((k + 1) // 2)) % 8
 
     def to_others(send):
-        def at_cell(k, _):
+        for k in range(7):
             to_cell = away(k)
             for to_tm in planes:
                 send(to_cell, to_tm)
-            return 0
-
-        lax.fori_loop(0, 7, at_cell, 0)
         for to_tm in planes[:15]:
             send(cell, to_tm)
 

time: 86.5 us -> 86.6 us (level)
  no operation moved by 1% of the time
where the time goes in v9:
time: 86.6 us; the launch traced here: 86.4 us
  Pallas kernels  84.4 us (97%)
  other arithmetic  1.25 us (1%)
    pallas_call x1, Pallas kernels, whole(): pl.pallas_call(main_kernel, out_shape=(row, row, row), in_specs=[vmem] *...  82.1 us
    pallas_call x1, Pallas kernels, prep(): pl.pallas_call(prep_kernel, out_shape=(jax.ShapeDtypeStruct((CAP, DEV), j...  2.27 us

profile of v9, /device:TPU:1, one launch (start us, length us, event | category | flops | bytes accessed | tf_op | source)
XLA Modules:
  0.0 86.4 jit_solution(6383807078549959874)
XLA Ops:
  0.6 0.0 copy-start.1
  0.6 0.0 copy-start
  0.7 0.0 copy-start.2
  0.7 2.3 %prep.1 = (s32[32,128]{1,0:T(8,128)}, f32[1,2048]{1,0:T(1,128)}) custom-call(s32[1,2048]{1,0:T(1,128)} %bitcast.10), custom_call_target="tpu_custom_call" | custom-call | tf_op jit(solution)/shard_map/prep/pallas_call | solution.py:73
  2.9 82.1 %whole.1 = (f32[1,256]{1,0:T(1,128)}, f32[1,256]{1,0:T(1,128)}, f32[1,256]{1,0:T(1,128)}) custom-call(f32[1,256]{1,0:T(1,128)} %bitcast.15, f32[1,256]{1,0:T(1,128)} %bitcast.16, f32[1,256]{1,0:T(1,128)} %bitcast.17, s32[1,2048]{1,0:T(1,128)} %bitcast.11, s32[1,2048]{1,0:T(1,128)} %bitcast.12, s32[1,2048]{1,0:T(1,128)} %bitcast.13, s32[1,2048]{1,0:T(1,128)} %bitcast.14, ...), custom_call_target="tpu_custom_call" | custom-call | tf_op jit(solution)/shard_map/whole/pallas_call | solution.py:579
  85.1 0.0 copy-done.1
  85.1 0.0 copy-done
  85.1 0.0 copy-done.2
  85.1 1.2 %multiply_add_fusion = (f32[256]{0:T(256)}, f32[256]{0:T(256)}, f32[256]{0:T(256)}) fusion(f32[256]{0:T(256)} %bitcast.20, f32[256]{0:T(256)S(1)} %copy-done.1, f32[256]{0:T(256)S(1)} %copy-done, f32[256]{0:T(256)} %bitcast.19, f32[256]{0:T(256)} %bitcast.18, f32[256]{0:T(256)S(1)} %copy-done.2), kind=kLoop, calls=%fused_computation | loop fusion | flops 1536 | bytes 9216 | tf_op jit(solution)/shard_map/add | solution.py:676
Async XLA Ops:
  0.6 84.5 %copy-start.1 = (f32[256]{0:T(256)S(1)}, f32[256]{0:T(256)}, u32[]{:S(2)}) copy-start(f32[256]{0:T(256)} %param.13) | copy-start | bytes 3076
  0.6 84.5 %copy-start = (f32[256]{0:T(256)S(1)}, f32[256]{0:T(256)}, u32[]{:S(2)}) copy-start(f32[256]{0:T(256)} %param.12) | copy-start | bytes 3076
  0.7 84.5 %copy-start.2 = (f32[256]{0:T(256)S(1)}, f32[256]{0:T(256)}, u32[]{:S(2)}) copy-start(f32[256]{0:T(256)} %param.11) | copy-start | bytes 3076
